TPU v7x, 8 devices: a whole 2x2x1 slice. The times are simulated.
8 devices in a mesh: dp: 8 (over z, y, x, core).
Axes of the slice: x: 2, y: 2, z: 1, core: 2. Of those that a mesh axis runs over, the one named last changes fastest.
Arguments:
- grad_embed: bfloat16 [8, 4096, 3840], P('dp')
- grad_q: bfloat16 [8, 6, 3840, 64], P('dp')
- grad_k: bfloat16 [8, 6, 3840, 32], P('dp')
- grad_v: bfloat16 [8, 6, 3840, 32], P('dp')
- grad_out: bfloat16 [8, 6, 64, 3840], P('dp')
- grad_gate: bfloat16 [8, 6, 3840, 240], P('dp')
- grad_up: bfloat16 [8, 6, 3840, 240], P('dp')
- grad_down: bfloat16 [8, 6, 240, 3840], P('dp')
- grad_norms: bfloat16 [8, 6, 4, 3840], P('dp')
- grad_qk_norms: bfloat16 [8, 6, 2, 256], P('dp')
- first_moment: float32 [36836352], P('dp')
- second_moment: float32 [36836352], P('dp')
- master_param: float32 [36836352], P('dp')
- hyper_params: float32 [5], replicated
Outputs:
- output 1: bfloat16 [4096, 3840], replicated
- output 2: bfloat16 [6, 3840, 64], replicated
- output 3: bfloat16 [6, 3840, 32], replicated
- output 4: bfloat16 [6, 3840, 32], replicated
- output 5: bfloat16 [6, 64, 3840], replicated
- output 6: bfloat16 [6, 3840, 240], replicated
- output 7: bfloat16 [6, 3840, 240], replicated
- output 8: bfloat16 [6, 240, 3840], replicated
- output 9: bfloat16 [6, 4, 3840], replicated
- output 10: bfloat16 [6, 2, 256], replicated
- output 11: float32 [36836352], P('dp')
- output 12: float32 [36836352], P('dp')
- output 13: float32 [36836352], P('dp')
All inputs are finite; a program needn't handle non-finite values.
Results may differ from a plain program's by a relative error of at most 0.001.
Values are sent between devices in bfloat16 or wider.
A program may use at most 1 GiB of HBM per device.

v0:
```python
import math
import jax
import jax.numpy as jnp
from jax import lax
from jax.sharding import PartitionSpec as P

ADAM_STEP = 7
ADAM_EPS = 1e-8
CLIP_EPS = 1e-6
GRAD_COUNT = 10
NORM_COUNT = 2


def adam_step(grad_part, first_part, second_part, master_part, hyper_params, clip_scale, keep_decay):
    learn_rate = hyper_params[0]
    beta_one = hyper_params[1]
    beta_two = hyper_params[2]
    weight_decay = hyper_params[3]
    clipped = grad_part * clip_scale
    moment_one = beta_one * first_part + (1.0 - beta_one) * clipped
    moment_two = beta_two * second_part + (1.0 - beta_two) * (clipped * clipped)
    m_hat = moment_one / (1.0 - beta_one ** ADAM_STEP)
    v_hat = moment_two / (1.0 - beta_two ** ADAM_STEP)
    direction = m_hat / (jnp.sqrt(v_hat) + ADAM_EPS) + jnp.where(keep_decay, weight_decay * master_part, 0.0)
    new_master = master_part - learn_rate * direction
    return moment_one, moment_two, new_master


def split_params(joined, shapes):
    pieces = []
    start_pos = 0
    for tensor_dims in shapes:
        tensor_size = math.prod(tensor_dims)
        pieces.append(joined[start_pos:start_pos + tensor_size].reshape(tensor_dims))
        start_pos = start_pos + tensor_size
    return pieces


def solution(mesh):
    group_size = mesh.shape["dp"]

    def local_update(*arrays):
        grads = arrays[:GRAD_COUNT]
        first_part, second_part, master_part, hyper_params = arrays[GRAD_COUNT:]
        shapes = [grad_arr.shape[1:] for grad_arr in grads]
        sizes = [math.prod(tensor_dims) for tensor_dims in shapes]
        total_len = sum(sizes)
        shard_len = total_len // group_size
        decay_len = total_len - sum(sizes[GRAD_COUNT - NORM_COUNT:])
        local_vec = jnp.concatenate([grad_arr.reshape(-1) for grad_arr in grads]).reshape(group_size, shard_len)
        received = lax.all_to_all(local_vec, "dp", 0, 0, tiled=True)
        grad_part = jnp.sum(received, axis=0, dtype=jnp.float32) / group_size
        square_sum = lax.psum(jnp.sum(grad_part * grad_part), "dp")
        clip_scale = jnp.minimum(1.0, hyper_params[4] / (jnp.sqrt(square_sum) + CLIP_EPS))
        offset = lax.axis_index("dp") * shard_len
        keep_decay = offset + lax.broadcasted_iota(jnp.int32, (shard_len,), 0) < decay_len
        moment_one, moment_two, new_master = adam_step(grad_part, first_part, second_part, master_part, hyper_params, clip_scale, keep_decay)
        full_vec = lax.all_gather(new_master.astype(jnp.bfloat16), "dp", tiled=True)
        return tuple(split_params(full_vec, shapes)) + (moment_one, moment_two, new_master)

    in_specs = tuple([P("dp")] * GRAD_COUNT + [P("dp"), P("dp"), P("dp"), P()])
    out_specs = tuple([P()] * GRAD_COUNT + [P("dp"), P("dp"), P("dp")])
    return jax.shard_map(local_update, mesh=mesh, in_specs=in_specs, out_specs=out_specs, check_vma=False)
```

profile of v0, /device:TPU:0, one launch (start us, length us, event | category | flops | bytes accessed | tf_op | source)
XLA Modules:
  0.0 4869.8 jit_solution(13124491795995345704)
XLA Ops:
  7.2 58.8 %reshape.97 = bf16[15728640]{0:T(1024)(128)(2,1)} reshape(bf16[1,4096,3840]{2,1,0:T(8,128)(2,1)} %param.14) | data formatting | bytes 62914560 | tf_op jit(solution)/shard_map/reshape | solution.py:50
  66.0 21.5 constant_dynamic-update-slice_fusion.9
  148.6 28.8 reshape.102
  193.3 28.8 reshape.103
  222.1 21.3 reshape.104
  276.2 166.2 %while.2 = (u32[]{:T(128)}, bf16[36836352]{0:T(1024)(128)(2,1)}, bf16[8,1,4604544]{2,1,0:T(2,128)(2,1)}, u32[]{}, u32[]{}) while((u32[]{:T(128)}, bf16[36836352]{0:T(1024)(128)(2,1)}, bf16[8,1,4604544]{2,1,0:T(2,128)(2,1)}, u32[]{}, u32[]{}) %tuple.37), condition=%wide.cond, body=%wide.body.sunk | while | flops 9 | bytes 46045604
  442.8 451.8 %reduce.2 = bf16[8,4604544]{1,0:T(8,128)(2,1)} reduce(bf16[8,1,4604544]{2,1,0:T(2,128)(2,1)} %get-tuple-element.43, bf16[]{:T(256)} %broadcast.3), dimensions={1}, to_apply=%get-tuple-element.43.reduce_sub_computation | reduce | bytes 147345408 | tf_op jit(solution)/shard_map/all_to_all | solution.py:51
  894.6 433.5 %reshape.121 = bf16[8,2,2302272]{2,1,0:T(2,128)(2,1)} reshape(bf16[8,4604544]{1,0:T(8,128)(2,1)} %reduce.2) | data formatting | bytes 147345408
  1343.2 789.5 %all-to-all-done = bf16[8,2,2302272]{2,1,0:T(2,128)(2,1)} async-done(((bf16[8,2,2302272]{2,1,0:T(2,128)(2,1)}), bf16[8,2,2302272]{2,1,0:T(2,128)(2,1)}, u32[]{:S(2)}, u32[]{:S(2)}) %all-to-all-start) | async-done | bytes 73672736 | tf_op jit(solution)/shard_map/all_to_all | solution.py:51
  2132.8 185.1 %reshape.122 = bf16[8,1,4604544]{2,1,0:T(2,128)(2,1)} reshape(bf16[8,2,2302272]{2,1,0:T(2,128)(2,1)} %all-to-all-done) | data formatting | bytes 147345408
  2317.9 767.3 %convert_reduce_fusion = f32[4604544]{0:T(1024)} fusion(bf16[8,1,4604544]{2,1,0:T(2,128)(2,1)} %reshape.122), kind=kLoop, calls=%fused_computation | loop fusion | flops 69068160 | bytes 92090880 | tf_op jit(solution)/shard_map/reduce_sum | solution.py:52
  3095.0 22.4 psum.7
  3118.7 51.1 %fusion = (bf16[4604544]{0:T(1024)(128)(2,1)}, f32[4604544]{0:T(1024)}, f32[4604544]{0:T(1024)}, f32[4604544]{0:T(1024)}) fusion(f32[4604544]{0:T(1024)} %param.26, f32[]{:T(128)} %bitcast.4, s32[]{:T(128)S(6)} %mul.99, f32[]{:T(128)S(6)} %sub.18, f32[]{:T(128)S(6)} %sub.16, f32[]{:T(128)} %bitcast, f32[4604544]{0:T(1024)} %convert_reduce_fusion, ...), kind=kLoop, calls=%fused_computation.16 | loop fusion | flops 92090880 | bytes 138136352 | tf_op jit(solution)/shard_map/convert_element_type | solution.py:58
  3169.9 18.2 while.1
  3188.1 638.5 %all-gather.3.cloned.1.call-done = bf16[8,1,4604544]{2,1,0:T(2,128)(2,1)} async-done(((bf16[1,1,4604544]{2,1,0:T(2,128)(2,1)}), bf16[8,1,4604544]{2,1,0:T(2,128)(2,1)}) %all-gather.3.cloned.1.call-update) | async-done | bytes 73672720 | tf_op jit(solution)/shard_map/all_gather | solution.py:58
  3826.6 451.3 %reduce.1 = bf16[8,4604544]{1,0:T(8,128)(2,1)} reduce(bf16[8,1,4604544]{2,1,0:T(2,128)(2,1)} %all-gather.3.cloned.1.call-done, bf16[]{:T(256)} %constant.29), dimensions={1}, to_apply=%all-gather.reduce_sub_computation | reduce | bytes 147345408 | tf_op jit(solution)/shard_map/all_gather | solution.py:58
  4277.9 326.1 %reshape.117 = bf16[36836352]{0:T(1024)(128)(2,1)} reshape(bf16[8,4604544]{1,0:T(8,128)(2,1)} %reduce.1) | data formatting | bytes 147345408
  4604.0 21.3 slice.71
  4633.0 21.7 fusion.1
  4654.7 56.1 %reshape.107 = bf16[4096,3840]{1,0:T(8,128)(2,1)} reshape(bf16[15728640]{0:T(1024)(128)(2,1)} %slice.71) | data formatting | bytes 62914560 | tf_op jit(solution)/shard_map/reshape | solution.py:34
  4757.0 25.9 reshape.112
  4798.9 25.9 reshape.113
  4824.8 16.1 copy.47
  4840.9 20.3 reshape.114
  (84 shorter events, 385.0 us)
Async XLA Ops:
  65.9 21.8 copy-start
  193.3 50.1 %copy-start.1 = (bf16[1,6,4,3840]{3,2,1,0:T(4,128)(2,1)S(1)}, bf16[1,6,4,3840]{3,2,1,0:T(4,128)(2,1)}, u32[]{:S(2)}) copy-start(bf16[1,6,4,3840]{3,2,1,0:T(4,128)(2,1)} %param.22) | copy-start | bytes 552964
  193.3 50.2 %copy-start.3 = (bf16[1,6,2,256]{3,2,1,0:T(2,128)(2,1)S(1)}, bf16[1,6,2,256]{3,2,1,0:T(2,128)(2,1)}, u32[]{:S(2)}) copy-start(bf16[1,6,2,256]{3,2,1,0:T(2,128)(2,1)} %param.23) | copy-start | bytes 18436
  245.3 19.9 slice-start.2
  250.7 14.5 slice-start.3
  253.9 11.3 slice-start.4
  253.9 16.2 slice-start.5
  253.9 16.2 slice-start.6
  265.2 4.8 slice-start.7
  1328.1 9.3 copy-start.2
  1328.1 804.7 %all-to-all-start = ((bf16[8,2,2302272]{2,1,0:T(2,128)(2,1)}), bf16[8,2,2302272]{2,1,0:T(2,128)(2,1)}, u32[]{:S(2)}, u32[]{:S(2)}) async-start(bf16[8,2,2302272]{2,1,0:T(2,128)(2,1)} %reshape.121), calls=%async_computation | async-start | bytes 147349504 | tf_op jit(solution)/shard_map/all_to_all | solution.py:51
  1337.4 2489.2 %all-gather.3.cloned.1.call-start = ((), (), s32[]{:S(2)}) async-start(), calls=%async_computation.1 | async-start | bytes 165763584 | tf_op jit(solution)/shard_map/all_gather | solution.py:58
  4824.8 36.4 slice-start
  4824.8 37.1 slice-start.1
Sparse Core Ops, SparseCore 0:
  3188.2 638.3 all-gather.2
where the time goes:
time: 4890 us; the launch traced here: 4870 us
  other arithmetic  1730 us (35%)
  local copies, waits for them, and re-layouts  1660 us (34%)
  waiting for transfers between devices  1430 us (29%)
    unnamed x61, local copies, waits for them, and re-layouts  1280 us
    all_to_all x1, waiting for transfers between devices, local_update(): received = lax.all_to_all(local_vec, 'dp', 0, 0, tiled=True)  790 us
    reduce_sum x1, other arithmetic, local_update(): grad_part = jnp.sum(received, axis=0, dtype=jnp.float32) / group_size  767 us
    all_gather x1, waiting for transfers between devices, local_update(): full_vec = lax.all_gather(new_master.astype(jnp.bfloat16), 'dp', tiled=True)  638 us
    all_to_all x1, other arithmetic, local_update(): received = lax.all_to_all(local_vec, 'dp', 0, 0, tiled=True)  452 us
    all_gather x1, other arithmetic, local_update(): full_vec = lax.all_gather(new_master.astype(jnp.bfloat16), 'dp', tiled=True)  451 us
    reshape x9, local copies, waits for them, and re-layouts, local_update(): grad_arr.reshape(-1)  167 us
    reshape x9, local copies, waits for them, and re-layouts, split_params(): joined[start_pos:start_pos + tensor_size].reshape(tensor_dims)  156 us
  transfers between devices with their start and end apart: 2, of which 2 were waited for; matrix products, arithmetic and copies ran while one was open for 0% of the time, Pallas kernels for 0%

commit v1 on v0

v1 whole, which is shorter than its diff:
```python
import functools
import math

import jax
import jax.numpy as jnp
import numpy as np
from jax import lax
from jax.experimental import pallas as pl
from jax.experimental.pallas import tpu as pltpu
from jax.sharding import PartitionSpec as P

ADAM_STEP = 7
ADAM_EPS = 1e-8
CLIP_EPS = 1e-6
D = 3840
BLK = D // 128
LAYERS = 6
DEV = 8
TENSORS = (("R", 4096, 1), ("C", 64, LAYERS), ("C", 32, LAYERS), ("C", 32, LAYERS), ("R", 64 * LAYERS, 1),
           ("C", 240, LAYERS), ("C", 240, LAYERS), ("R", 240 * LAYERS, 1))
SIZES = tuple(rows * layers * D for _, rows, layers in TENSORS)
STARTS = tuple(sum(SIZES[:i]) for i in range(len(SIZES)))
DECAY = sum(SIZES)
TAIL = LAYERS * 4 * D + LAYERS * 2 * 256
TOTAL = DECAY + TAIL
SHARE = TOTAL // DEV
SROWS = SHARE // 128
NT = 4536
NR = NT * 8
GUARD = 240
NCH = 9
CR = NR // 2 // NCH
MESH = pl.DeviceIdType.MESH


def plan():
    pieces, units = [], []
    for r in range(DEV):
        lo, hi = r * SHARE, (r + 1) * SHARE
        off, plist, ulist = 0, [], []
        for t, (kind, rows, layers) in enumerate(TENSORS):
            if kind == "R":
                a, b = max(lo, STARTS[t]), min(hi, STARTS[t] + SIZES[t])
                if a >= b:
                    continue
                g0, g1 = (a - STARTS[t]) // (8 * D), -((STARTS[t] - b) // (8 * D))
                plist.append((t, 0, g0, g1, off))
                for g in range(g0, g1):
                    ulist.append(("R", off + (g - g0) * BLK, 1, (STARTS[t] + g * 8 * D - lo) // 128))
                off += (g1 - g0) * BLK
                continue
            for l in range(layers):
                s = STARTS[t] + l * rows * D
                a, b = max(lo, s), min(hi, s + rows * D)
                if a >= b:
                    continue
                j0, j1 = (a - s) // (128 * rows), -((s - b) // (128 * rows))
                plist.append((t, l, j0, j1, off))
                for j in range(j0, j1):
                    ulist.append((rows, off + j - j0, j1 - j0, (s + j * 128 * rows - lo) // 128))
                off += (j1 - j0) * rows // 8
        if hi > DECAY:
            for i in range(TAIL // 1024):
                ulist.append(("T", off + i, 1, (DECAY - lo) // 128 + 8 * i))
            plist.append((len(TENSORS), 0, 0, TAIL // 1024, off))
            off += TAIL // 1024
        assert off <= NT
        pieces.append((plist, off))
        units.append(ulist)
    return pieces, units


PIECES, UNITS = plan()


def flip(dev, bit):
    return dev + bit - 2 * bit * (lax.rem(lax.div(dev, bit), 2))


def barrier_all(me):
    sem = pltpu.get_barrier_semaphore()
    for step in range(1, DEV):
        pl.semaphore_signal(sem, inc=1, device_id=(lax.rem(me + step, DEV),), device_id_type=MESH)
    pl.semaphore_wait(sem, DEV - 1)


def rs_kernel(s_ref, g_ref, sq_ref, r_ref, part, land, loads, outs, accum, sq_all,
              send1, recv1, send2, recv2, load_sem, out_sem, sq_send, sq_recv):
    me = lax.axis_index("dp")
    barrier_all(me)
    half = NR // 2

    def hop(d, q, slot, k):
        first, second = (2, 4) if d == 0 else (4, 2)
        target = flip(me, 1) if slot == 0 else flip(me, first) if slot == 1 else flip(flip(me, first), 1)
        owner = flip(target, second) if q == 0 else target
        return pltpu.make_async_remote_copy(
            src_ref=s_ref.at[pl.ds(owner * NR + d * half + k * CR, CR)],
            dst_ref=r_ref.at[pl.ds(((d * 2 + q) * 3 + slot) * half + k * CR, CR)],
            send_sem=send1.at[d, q, slot, k], recv_sem=recv1.at[d, q, slot, k],
            device_id=(target,), device_id_type=MESH)

    def pass_on(d, k):
        second = 4 if d == 0 else 2
        return pltpu.make_async_remote_copy(
            src_ref=part.at[pl.ds(d * half + k * CR, CR)], dst_ref=land.at[pl.ds(d * half + k * CR, CR)],
            send_sem=send2.at[d, k], recv_sem=recv2.at[d, k],
            device_id=(flip(me, second),), device_id_type=MESH)

    for q in range(2):
        @pl.loop(0, NCH)
        def _(k):
            for slot in (1, 2, 0):
                for d in range(2):
                    hop(d, q, slot, k).start()

    def load(d, q, slot, k, buf):
        second = 4 if d == 0 else 2
        if slot == 3:
            owner = flip(me, second) if q == 0 else me
            src = s_ref.at[pl.ds(owner * NR + d * half + k * CR, CR)]
        else:
            src = r_ref.at[pl.ds(((d * 2 + q) * 3 + slot) * half + k * CR, CR)]
        return pltpu.make_async_copy(src, loads.at[buf, slot], load_sem.at[buf, slot])

    def fetch(d, q, k, buf):
        for slot in range(3):
            hop(d, q, slot, k).wait_recv()
        for slot in range(4):
            load(d, q, slot, k, buf).start()

    def ready(d, q, k, buf):
        for slot in range(4):
            load(d, q, slot, k, buf).wait()

    def total(buf, rows):
        acc = loads[buf, 3, rows, :].astype(jnp.float32)
        for slot in range(3):
            acc = acc + loads[buf, slot, rows, :].astype(jnp.float32)
        return acc

    STEP = 112

    for d in range(2):
        fetch(d, 0, 0, d)

    @pl.loop(0, NCH)
    def _(k):
        for d in range(2):
            ready(d, 0, k, d)

            @pl.loop(0, CR // STEP)
            def _(i):
                rows = pl.ds(i * STEP, STEP)
                part[pl.ds(d * half + k * CR + i * STEP, STEP), :] = total(d, rows)

            @pl.when(k + 1 < NCH)
            def _():
                fetch(d, 0, k + 1, d)

            pass_on(d, k).start()

    accum[...] = jnp.zeros_like(accum)
    skip_rows = me * 0

    def out_copy(d, k):
        return pltpu.make_async_copy(outs.at[d], g_ref.at[pl.ds(d * half + k * CR, CR)], out_sem.at[d])

    for d in range(2):
        fetch(d, 1, 0, d)

    @pl.loop(0, NCH)
    def _(k):
        for d in range(2):
            ready(d, 1, k, d)
            pass_on(d, k).wait_recv()

            @pl.when(k > 0)
            def _():
                out_copy(d, k - 1).wait()

            @pl.loop(0, CR // STEP)
            def _(i):
                base = d * half + k * CR + i * STEP
                g = (total(d, pl.ds(i * STEP, STEP)) + land[pl.ds(base, STEP), :]) * (1.0 / DEV)
                outs[d, pl.ds(i * STEP, STEP), :] = g
                tile = lax.div(base, 8) + lax.broadcasted_iota(jnp.int32, (STEP // 8, 8, 128), 0)
                g3 = g.reshape(STEP // 8, 8, 128)
                accum[...] += jnp.sum(jnp.where(counted(me, tile), g3 * g3, 0.0), axis=0)

            @pl.when(k + 1 < NCH)
            def _():
                fetch(d, 1, k + 1, d)

            out_copy(d, k).start()

    sq_all[pl.ds(me * 8, 8), :] = accum[...]
    for d in range(2):
        out_copy(d, NCH - 1).wait()
    for d in range(2):
        @pl.loop(0, NCH)
        def _(k):
            for q in range(2):
                for slot in range(3):
                    hop(d, q, slot, k).wait_send()
            pass_on(d, k).wait_send()

    def tell(step):
        return pltpu.make_async_remote_copy(
            src_ref=accum, dst_ref=sq_all.at[pl.ds(me * 8, 8)],
            send_sem=sq_send.at[step], recv_sem=sq_recv.at[step],
            device_id=(lax.rem(me + step + 1, DEV),), device_id_type=MESH)

    for step in range(DEV - 1):
        tell(step).start()
    for step in range(DEV - 1):
        tell(step).wait()
    whole = sq_all[pl.ds(0, 8), :]
    for i in range(1, DEV):
        whole = whole + sq_all[pl.ds(8 * i, 8), :]
    sq_ref[...] = jnp.broadcast_to(jnp.sum(whole, keepdims=True), (8, 128))


def shared_first():
    found = []
    for r in range(1, DEV):
        kind, tile, stride, row = UNITS[r][0]
        if row >= 0:
            continue
        found.append((r, BLK, 1) if kind == "R" else (r, stride * kind // 8, stride))
    return found


def counted(me, tile):
    keep = tile >= 0
    for r, tiles, period in shared_first():
        skip = (tile < tiles) & (lax.rem(tile, period) == 0)
        keep = keep & jnp.logical_not(skip & (me == r))
    return keep


def reduce_scatter(send):
    half = NR // 2
    return pl.pallas_call(
        rs_kernel,
        name="reduce_scatter",
        out_shape=(jax.ShapeDtypeStruct((NR, 128), jnp.float32), jax.ShapeDtypeStruct((8, 128), jnp.float32),
                   jax.ShapeDtypeStruct((12 * half, 128), jnp.bfloat16)),
        in_specs=[pl.BlockSpec(memory_space=pl.ANY)],
        out_specs=(pl.BlockSpec(memory_space=pl.ANY), pl.BlockSpec(memory_space=pltpu.VMEM),
                   pl.BlockSpec(memory_space=pl.ANY)),
        scratch_shapes=[
            pltpu.VMEM((NR, 128), jnp.float32), pltpu.VMEM((NR, 128), jnp.float32),
            pltpu.VMEM((2, 4, CR, 128), jnp.bfloat16), pltpu.VMEM((2, CR, 128), jnp.float32),
            pltpu.VMEM((8, 128), jnp.float32), pltpu.VMEM((8 * DEV, 128), jnp.float32),
            pltpu.SemaphoreType.DMA((2, 2, 3, NCH)), pltpu.SemaphoreType.DMA((2, 2, 3, NCH)),
            pltpu.SemaphoreType.DMA((2, NCH)), pltpu.SemaphoreType.DMA((2, NCH)),
            pltpu.SemaphoreType.DMA((2, 4)), pltpu.SemaphoreType.DMA((2,)),
            pltpu.SemaphoreType.DMA((DEV - 1,)), pltpu.SemaphoreType.DMA((DEV - 1,))],
        compiler_params=pltpu.CompilerParams(collective_id=0, has_side_effects=True, vmem_limit_bytes=60 << 20),
    )(send)


BR = 1128
NB = -(-SROWS // BR)
KINDS = ("R", 240, 64, 32, "T")


def unit_tables():
    depth = max(len([u for u in ulist if u[0] == kind]) for ulist in UNITS for kind in KINDS)
    entry = np.zeros((DEV, len(KINDS), 3, depth), np.int32)
    span = np.zeros((DEV, len(KINDS), 2, NB + 1), np.int32)
    for r, ulist in enumerate(UNITS):
        for n, kind in enumerate(KINDS):
            mine = [u for u in ulist if u[0] == kind]
            length = 8 if kind == "T" else 240 if kind == "R" else kind
            for i, u in enumerate(mine):
                entry[r, n, :, i] = (u[1] * 8, u[2] * 8, u[3] + GUARD)
            for b in range(NB):
                span[r, n, 0, b + 1] = sum(u[3] < (b + 1) * BR for u in mine)
                span[r, n, 1, b + 1] = sum(u[3] + length <= (b + 1) * BR for u in mine) if b < NB - 1 else len(mine)
    return entry, span, depth


ENTRY, SPAN, DEPTH = unit_tables()


def lanes(rows):
    return lax.broadcasted_iota(jnp.int32, (rows, 128), 1)


def roll(x, shift):
    shift = shift % 128
    return x if shift == 0 else pltpu.roll(x, shift, 1)


def to_flat(kind, tiles, flat, ta, tb, base, stride, row):
    def tile(i):
        return tiles[pl.ds(pl.multiple_of(base + i * stride, 8), 8), :]

    if kind == "T":
        flat[pl.ds(row, 8), :] = tile(0)
        return
    if kind == "R":
        for c in range(BLK):
            flat[pl.ds(row + c, 8, stride=BLK), :] = tile(c)
        return
    count = kind // 8
    grid = jnp.concatenate([tile(i) for i in range(min(count, 16))], axis=0)
    if count < 16:
        grid = jnp.concatenate([grid, jnp.zeros((128 - kind, 128), jnp.float32)], axis=0)
    ta[...] = grid.T
    if kind == 240:
        grid = jnp.concatenate([tile(i) for i in range(16, 30)] + [jnp.zeros((16, 128), jnp.float32)], axis=0)
        tb[...] = grid.T
        lane = lanes(16)
        for k in range(15):
            r, o = divmod(128 * k, 240)
            if o < 128:
                x = ta[pl.ds(r, 16, stride=8), :]
                if o > 0:
                    x = jnp.where(lane >= o, x, tb[pl.ds(r, 16, stride=8), :])
            else:
                x = tb[pl.ds(r, 16, stride=8), :]
            x = roll(x, -o)
            if o + 128 > 240:
                x = jnp.where(lane >= 240 - o, roll(ta[pl.ds(r + 1, 16, stride=8), :], 240 - o), x)
            flat[pl.ds(row + k, 16, stride=15), :] = x
        return
    per = 128 // kind
    lane = lanes(kind)
    x = ta[pl.ds(0, kind, stride=per), :]
    for q in range(1, per):
        x = jnp.where(lane >= q * kind, roll(ta[pl.ds(q, kind, stride=per), :], q * kind), x)
    flat[pl.ds(row, kind), :] = x


def to_tiles(kind, tiles, flat, ta, tb, base, stride, row):
    def put(i, value):
        tiles[pl.ds(pl.multiple_of(base + i * stride, 8), 8), :] = value

    if kind == "T":
        put(0, flat[pl.ds(row, 8), :])
        return
    if kind == "R":
        for c in range(BLK):
            put(c, flat[pl.ds(row + c, 8, stride=BLK), :])
        return
    if kind == 240:
        lane = lanes(16)
        for r in range(8):
            k, o = divmod(240 * r, 128)
            f = [flat[pl.ds(row + k + i, 16, stride=15), :] for i in range(3 if k + 2 < 15 else 2)]
            first = f[0] if o == 0 else roll(jnp.where(lane >= o, f[0], f[1]), -o)
            second = f[1] if o == 0 else roll(jnp.where(lane >= o, f[1], f[2]) if len(f) > 2 else f[1], -o)
            ta[pl.ds(r, 16, stride=8), :] = first
            tb[pl.ds(r, 16, stride=8), :] = second
        grid = ta[...].T
        for i in range(16):
            put(i, grid[8 * i:8 * i + 8])
        grid = tb[...].T
        for i in range(14):
            put(16 + i, grid[8 * i:8 * i + 8])
        return
    per = 128 // kind
    f = flat[pl.ds(row, kind), :]
    for q in range(per):
        ta[pl.ds(q, kind, stride=per), :] = roll(f, -q * kind)
    grid = ta[...].T
    for i in range(kind // 8):
        put(i, grid[8 * i:8 * i + 8])


def adam_kernel(entry, span, scal, g_ref, sq_ref, m_ref, v_ref, p_ref, m_out, v_out, p_out, a_ref,
                tiles, flat, ta, tb, low, g_sem, a_sem):
    me = lax.axis_index("dp")
    b = pl.program_id(0)
    load = pltpu.make_async_copy(g_ref, tiles, g_sem)

    @pl.when(b == 0)
    def _():
        load.start()
        load.wait()

    def each(which, work):
        for n, kind in enumerate(KINDS):
            at = (n * 3) * DEPTH

            def body(u, carry, kind=kind, at=at):
                work(kind, tiles, flat, ta, tb, entry[me, at + u],
                     entry[me, at + DEPTH + u], entry[me, at + 2 * DEPTH + u])
                return carry

            first = (n * 2 + which) * (NB + 1) + b
            lax.fori_loop(span[me, first], span[me, first + 1], body, 0)

    each(0, to_flat)

    learn_rate, b1, c1, b2, c2, i1, i2, decay, max_norm = [scal[i] for i in range(9)]
    norm = jnp.sqrt(sq_ref[...])
    clip = jnp.minimum(1.0, max_norm / (norm + CLIP_EPS))[0:1, :]
    STEP = 24

    @pl.loop(0, BR // STEP)
    def _(i):
        rows = pl.ds(i * STEP, STEP)
        local = b * BR + i * STEP
        here = pl.ds(pl.multiple_of(GUARD + local, 8), STEP)
        h = flat[here, :] * clip
        m = b1 * m_ref[rows, :] + c1 * h
        v = b2 * v_ref[rows, :] + c2 * (h * h)
        p = p_ref[rows, :]
        m_out[rows, :] = m
        v_out[rows, :] = v
        where = me * SROWS + local + lax.broadcasted_iota(jnp.int32, (STEP, 128), 0)
        step = (m * i1) / (jnp.sqrt(v * i2) + ADAM_EPS) + jnp.where(where < DECAY // 128, decay * p, 0.0)
        p = p - learn_rate * step
        p_out[rows, :] = p
        flat[here, :] = p

    each(1, to_tiles)

    @pl.when(b == NB - 1)
    def _():
        @pl.loop(0, NR // 96)
        def _(i):
            rows = pl.ds(pl.multiple_of(i * 96, 96), 96)
            low[rows, :] = tiles[rows, :].astype(jnp.bfloat16)

        put = pltpu.make_async_copy(low, a_ref.at[pl.ds(pl.multiple_of(me * NR, 16), NR)], a_sem)
        put.start()
        put.wait()


def adam(scal, g, sq, m, v, p):
    block = pl.BlockSpec((BR, 128), lambda b, *_: (b, 0))
    anywhere = pl.BlockSpec(memory_space=pl.ANY)
    flat_shape = jax.ShapeDtypeStruct((SROWS, 128), jnp.float32)
    return pl.pallas_call(
        adam_kernel,
        name="adam",
        grid_spec=pltpu.PrefetchScalarGridSpec(
            num_scalar_prefetch=3, grid=(NB,),
            in_specs=[anywhere, pl.BlockSpec((8, 128), lambda b, *_: (0, 0)), block, block, block],
            out_specs=[block, block, block, anywhere],
            scratch_shapes=[
                pltpu.VMEM((NR, 128), jnp.float32), pltpu.VMEM((NB * BR + 2 * GUARD + 8, 128), jnp.float32),
                pltpu.VMEM((128, 128), jnp.float32), pltpu.VMEM((128, 128), jnp.float32),
                pltpu.VMEM((NR, 128), jnp.bfloat16), pltpu.SemaphoreType.DMA, pltpu.SemaphoreType.DMA]),
        out_shape=[flat_shape, flat_shape, flat_shape, jax.ShapeDtypeStruct((DEV * NR, 128), jnp.bfloat16)],
        compiler_params=pltpu.CompilerParams(dimension_semantics=("arbitrary",), vmem_limit_bytes=63 << 20),
    )(jnp.asarray(ENTRY.reshape(DEV, -1)), jnp.asarray(SPAN.reshape(DEV, -1)), scal, g, sq, m, v, p)


def ag_kernel(a_in, a_ref, send, recv):
    del a_in
    me = lax.axis_index("dp")
    barrier_all(me)
    half = NR // 2
    xn, yn, pn = flip(me, 2), flip(me, 4), flip(me, 1)
    diag = flip(xn, 4)

    def copy(kind, d, k):
        owner = (me, me, me, xn if d == 0 else yn, xn, yn, diag)[kind]
        target = (xn, yn, pn, yn if d == 0 else xn, pn, pn, pn)[kind]
        part = a_ref.at[pl.ds(owner * NR + d * half + k * CR, CR)]
        return pltpu.make_async_remote_copy(
            src_ref=part, dst_ref=part, send_sem=send.at[kind, d, k], recv_sem=recv.at[kind, d, k],
            device_id=(target,), device_id_type=MESH)

    for turn in range(2):
        @pl.loop(0, NCH)
        def _(k):
            copy(0, turn, k).start()
            copy(1, 1 - turn, k).start()
            copy(2, turn, k).start()

    @pl.loop(0, NCH)
    def _(k):
        copy(0, 0, k).wait_recv()
        copy(3, 0, k).start()
        copy(4, 0, k).start()
        copy(1, 1, k).wait_recv()
        copy(3, 1, k).start()
        copy(5, 1, k).start()

    @pl.loop(0, NCH)
    def _(k):
        copy(0, 1, k).wait_recv()
        copy(4, 1, k).start()
        copy(1, 0, k).wait_recv()
        copy(5, 0, k).start()

    @pl.loop(0, NCH)
    def _(k):
        for d in range(2):
            copy(3, d, k).wait_recv()
            copy(6, d, k).start()

    @pl.loop(0, NCH)
    def _(k):
        for d in range(2):
            for kind in (2, 4, 5, 6):
                copy(kind, d, k).wait_recv()
            for kind in range(7):
                copy(kind, d, k).wait_send()


def all_gather(mine):
    anywhere = pl.BlockSpec(memory_space=pl.ANY)
    return pl.pallas_call(
        ag_kernel,
        name="all_gather",
        out_shape=jax.ShapeDtypeStruct((DEV * NR, 128), jnp.bfloat16),
        in_specs=[anywhere], out_specs=anywhere,
        scratch_shapes=[pltpu.SemaphoreType.DMA((7, 2, NCH)), pltpu.SemaphoreType.DMA((7, 2, NCH))],
        input_output_aliases={0: 0},
        compiler_params=pltpu.CompilerParams(collective_id=1, has_side_effects=True),
    )(mine)


def as_tiles(t, x):
    kind, rows, layers = TENSORS[t]
    if kind == "C":
        x = jnp.swapaxes(x, -1, -2)
    return x.reshape(layers, rows // 8, 8, BLK, 128).transpose(0, 1, 3, 2, 4)


def from_tiles(t, x, shape):
    kind, rows, layers = TENSORS[t]
    x = x.transpose(0, 1, 3, 2, 4)
    if kind == "C":
        return jnp.swapaxes(x.reshape(layers, rows, D), -1, -2)
    return x.reshape(shape)


def pack(views, tail):
    parts = []
    for plist, used in PIECES:
        for t, l, first, last, _ in plist:
            if t == len(TENSORS):
                piece = tail
            elif TENSORS[t][0] == "R":
                piece = views[t][0, first:last]
            else:
                piece = views[t][l, :, first:last]
            parts.append(piece.reshape(-1, 128))
        if used < NT:
            parts.append(jnp.zeros(((NT - used) * 8, 128), jnp.bfloat16))
    return jnp.concatenate(parts, axis=0)


def join(left, right, start, row_step, col_step, tile_step, lane_step, bound):
    pos = start
    for axis, step in enumerate((row_step, col_step, tile_step, lane_step)):
        pos = pos + step * lax.broadcasted_iota(jnp.int32, left.shape, axis)
    return jnp.where(pos < bound, left, right)


def unpack(gathered, shapes):
    outs = []
    for t, (kind, rows, layers) in enumerate(TENSORS):
        per_layer = {}
        for r, (plist, _) in enumerate(PIECES):
            for pt, l, first, last, off in plist:
                if pt == t:
                    per_layer.setdefault(l, []).append((r, first, last, off))
        done = []
        for l in sorted(per_layer):
            axis = 0 if kind == "R" else 1
            parts = []
            for r, first, last, off in per_layer[l]:
                tiles = (last - first) * (BLK if kind == "R" else rows // 8)
                base = (r * NT + off) * 8
                shape = (last - first, BLK, 8, 128) if kind == "R" else (rows // 8, last - first, 8, 128)
                piece = gathered[base:base + tiles * 8].reshape(shape)
                if parts and first < parts[-1][2]:
                    start = STARTS[t] + (first * 8 * D if kind == "R" else l * rows * D + first * 128 * rows)
                    steps = (0, 128, D, 1) if kind == "R" else (8, 0, 1, rows)
                    prev = parts.pop()
                    size = prev[0].shape[axis]
                    left = lax.slice_in_dim(prev[0], size - 1, size, axis=axis)
                    right = lax.slice_in_dim(piece, 0, 1, axis=axis)
                    if size > 1:
                        parts.append((lax.slice_in_dim(prev[0], 0, size - 1, axis=axis), 0, 0))
                    parts.append((join(left, right, start, *steps, r * SHARE), 0, 0))
                    piece = lax.slice_in_dim(piece, 1, last - first, axis=axis)
                parts.append((piece, first, last))
            done.append(jnp.concatenate([p[0] for p in parts], axis=axis))
        whole = jnp.stack(done)
        if kind == "R":
            whole = whole.reshape(1, rows // 8, BLK, 8, 128)
        outs.append(from_tiles(t, whole, shapes[t]))
    plist, _ = PIECES[DEV - 1]
    off = plist[-1][4]
    tail = gathered[((DEV - 1) * NT + off) * 8:((DEV - 1) * NT + off) * 8 + TAIL // 128].reshape(-1)
    cut = math.prod(shapes[8])
    return outs + [tail[:cut].reshape(shapes[8]), tail[cut:].reshape(shapes[9])]


def solution(mesh):
    def local_update(*arrays):
        grads = arrays[:10]
        m, v, p, hyper = arrays[10:]
        shapes = [x.shape[1:] for x in grads]
        views = [as_tiles(t, grads[t][0]) for t in range(8)]
        tail = jnp.concatenate([grads[8].reshape(-1), grads[9].reshape(-1)])
        share, squares, _ = reduce_scatter(pack(views, tail))
        learn_rate, b1, b2, decay, max_norm = [hyper[i] for i in range(5)]
        scal = jnp.stack([learn_rate, b1, 1.0 - b1, b2, 1.0 - b2, 1.0 / (1.0 - b1 ** ADAM_STEP),
                          1.0 / (1.0 - b2 ** ADAM_STEP), decay, max_norm])
        m, v, p, mine = adam(scal, share, squares, *[x.reshape(SROWS, 128) for x in (m, v, p)])
        params = unpack(all_gather(mine), shapes)
        return tuple(params) + tuple(x.reshape(SHARE) for x in (m, v, p))

    in_specs = tuple([P("dp")] * 10 + [P("dp"), P("dp"), P("dp"), P()])
    out_specs = tuple([P()] * 10 + [P("dp"), P("dp"), P("dp")])
    return jax.shard_map(local_update, mesh=mesh, in_specs=in_specs, out_specs=out_specs, check_vma=False)
```

time: 4890 us -> 1380 us (0.28)
  other arithmetic: 1730 us -> 11.9 us
  local copies, waits for them, and re-layouts: 1660 us -> 199 us
  waiting for transfers between devices: 1430 us -> 0 us
  Pallas kernels: 0 us -> 1160 us
    unnamed x61 -> x105, local copies, waits for them, and re-layouts: 1280 us -> 107 us
    pallas_call x0 -> x3, Pallas kernels: none -> 1160 us  [the longest x1 615 us: reduce_scatter(): pl.pallas_call(rs_kernel, name='reduce_scatter', out_shape=(jax.ShapeDtyp...]
    all_to_all x1 -> x0, waiting for transfers between devices: 790 us -> none  [local_update(): received = lax.all_to_all(local_vec, 'dp', 0, 0, tiled=True)]
    reduce_sum x2 -> x0, other arithmetic: 777 us -> none  [the longest x1 767 us: local_update(): grad_part = jnp.sum(received, axis=0, dtype=jnp.float32) / group_size]
    all_gather x1 -> x0, waiting for transfers between devices: 638 us -> none  [local_update(): full_vec = lax.all_gather(new_master.astype(jnp.bfloat16), 'dp', tiled=True)]
    all_to_all x1 -> x0, other arithmetic: 452 us -> none  [local_update(): received = lax.all_to_all(local_vec, 'dp', 0, 0, tiled=True)]
    all_gather x1 -> x0, other arithmetic: 451 us -> none  [local_update(): full_vec = lax.all_gather(new_master.astype(jnp.bfloat16), 'dp', tiled=True)]
    reshape x18 -> x3, local copies, waits for them, and re-layouts: 324 us -> 1.41 us  [the longest x2 1.33 us: unpack(): return outs + [tail[:cut].reshape(shapes[8]), tail[cut:].reshape(shapes[9])]]
  transfers between devices with their start and end apart: 2 -> 0, of which waited for: 2 -> 0; matrix products, arithmetic and copies ran while one was open for 0% -> 0% of each run, Pallas kernels for 0% -> 0%
where the time goes in v1:
time: 1380 us; the launch traced here: 1370 us
  Pallas kernels  1160 us (84%)
  local copies, waits for them, and re-layouts  199 us (14%)
    pallas_call x1, Pallas kernels, reduce_scatter(): pl.pallas_call(rs_kernel, name='reduce_scatter', out_shape=(jax.ShapeDtyp...  615 us
    pallas_call x1, Pallas kernels, all_gather(): pl.pallas_call(ag_kernel, name='all_gather', out_shape=jax.ShapeDtypeStru...  461 us
    unnamed x105, local copies, waits for them, and re-layouts  107 us
    pallas_call x1, Pallas kernels, adam(): pl.pallas_call(adam_kernel, name='adam', grid_spec=pltpu.PrefetchScalarGr...  79.6 us
    slice x5, local copies, waits for them, and re-layouts, pack(): piece = views[t][0, first:last]  30.4 us

profile of v1, /device:TPU:0, one launch (start us, length us, event | category | flops | bytes accessed | tf_op | source)
XLA Modules:
  0.0 1373.8 jit_solution(15640420863880742399)
XLA Ops:
  9.3 8.9 slice.510
  18.1 9.1 constant_dynamic-update-slice_fusion.47
  27.8 8.5 fusion.22
  36.3 4.1 constant_dynamic-update-slice_fusion.45
  41.0 4.1 constant_dynamic-update-slice_fusion.43
  45.7 2.6 slice.513
  48.3 2.1 constant_dynamic-update-slice_fusion.41
  91.8 8.7 slice.548
  100.5 8.9 constant_dynamic-update-slice_fusion.1
  110.8 615.3 %reduce_scatter.1 = (f32[36288,128]{1,0:T(8,128)}, f32[8,128]{1,0:T(8,128)}, bf16[217728,128]{1,0:T(8,128)(2,1)}) custom-call(bf16[290304,128]{1,0:T(8,128)(2,1)} %constant_dynamic-update-slice_fusion.s_ref), custom_call_target="tpu_custom_call" | custom-call | tf_op jit(solution)/shard_map/reduce_scatter/pallas_call | solution.py:244
  726.1 79.6 %adam.1 = (f32[35973,128]{1,0:T(8,128)}, f32[35973,128]{1,0:T(8,128)}, f32[35973,128]{1,0:T(8,128)}, bf16[290304,128]{1,0:T(8,128)(2,1)}) custom-call(s32[8,4455]{1,0:T(8,128)} %constant.18.clone.entry, s32[8,330]{1,0:T(8,128)} %constant.19.clone.span, f32[9]{0:T(128)} %stack.49.scal, f32[36288,128]{1,0:T(8,128)} %get-tuple-element.19.g_ref, ...), custom_call_target="tpu_custom_call" | custom-call | tf_op jit(solution)/shard_map/adam/pallas_call | solution.py:439
  805.8 461.5 %all_gather.1 = bf16[290304,128]{1,0:T(8,128)(2,1)} custom-call(bf16[290304,128]{1,0:T(8,128)(2,1)} %get-tuple-element.21.a_in), custom_call_target="tpu_custom_call", output_to_operand_aliasing={{}: (0, {})} | custom-call | tf_op jit(solution)/shard_map/all_gather/pallas_call | solution.py:511
  1267.3 19.3 %fusion.21 = (bf16[35760,128]{1,0:T(8,128)(2,1)}, bf16[35760,128]{1,0:T(8,128)(2,1)}, bf16[35760,128]{1,0:T(8,128)(2,1)}) fusion(bf16[290304,128]{1,0:T(8,128)(2,1)} %all_gather.1), kind=kLoop, calls=%fused_computation.121 | loop fusion | bytes 54927360 | tf_op jit(solution)/shard_map/slice | solution.py:585
  1286.6 8.8 constant_dynamic-update-slice_fusion.54
  1297.0 8.8 constant_dynamic-update-slice_fusion.52
  1307.4 8.8 constant_dynamic-update-slice_fusion.50
  1317.9 2.2 slice.452
  1320.1 2.1 constant_dynamic-update-slice_fusion.48
  1326.2 2.2 fusion.18
  1332.9 3.1 slice.477
  1336.0 8.1 fusion.17
  1346.2 2.2 fusion.19
  1359.4 5.0 slice.506
  1366.2 4.6 pad_maximum_fusion
  (152 shorter events, 78.6 us)
Async XLA Ops:
  45.1 5.4 copy-start
  48.3 7.3 copy-start.3
  48.3 11.7 copy-start.2
  50.5 15.2 %copy-start.1 = (bf16[1,6,64,3840]{3,2,1,0:T(8,128)(2,1)S(1)}, bf16[1,6,64,3840]{3,2,1,0:T(8,128)(2,1)}, u32[]{:S(2)}) copy-start(bf16[1,6,64,3840]{3,2,1,0:T(8,128)(2,1)} %param.20) | copy-start | bytes 8847364
  51.5 15.8 %slice-start.3 = ((s8[11059200]{0:T(1024)(128)(4,1)}), s8[4194304]{0:T(1024)(128)(4,1)S(1)}, s32[]{:S(2)}) async-start(s8[11059200]{0:T(1024)(128)(4,1)} %bitcast.231), calls=%async_computation.3 | async-start | bytes 8388608
  55.6 11.7 slice-start.4
  62.3 5.0 slice-start.5
  68.0 9.7 slice-start
  70.7 6.9 slice-start.1
  73.6 4.0 slice-start.2
  100.5 8.9 copy-start.9
  100.5 8.9 copy-start.5
  1324.6 1.6 copy-start.6
  1328.7 1.1 copy-start.7
  1331.8 1.1 copy-start.8
  1353.5 5.9 copy-start.4

commit v2 on v1

--- a/solution.py
+++ b/solution.py
@@ -56,8 +56,10 @@
                     continue
                 j0, j1 = (a - s) // (128 * rows), -((s - b) // (128 * rows))
                 plist.append((t, l, j0, j1, off))
+                whole = j1 - j0 == BLK
                 for j in range(j0, j1):
-                    ulist.append((rows, off + j - j0, j1 - j0, (s + j * 128 * rows - lo) // 128))
+                    at, stride = (j, BLK) if whole else ((j - j0) * (rows // 8), 1)
+                    ulist.append((rows, off + at, stride, (s + j * 128 * rows - lo) // 128))
                 off += (j1 - j0) * rows // 8
         if hi > DECAY:
             for i in range(TAIL // 1024):
@@ -84,95 +86,171 @@
     pl.semaphore_wait(sem, DEV - 1)
 
 
-def rs_kernel(s_ref, g_ref, sq_ref, r_ref, part, land, loads, outs, accum, sq_all,
-              send1, recv1, send2, recv2, load_sem, out_sem, sq_send, sq_recv):
+def cut_layers():
+    return sorted({(t, l) for plist, _ in PIECES for t, l, a, b, _ in plist
+                   if t < len(TENSORS) and TENSORS[t][0] == "C" and b - a < BLK})
+
+
+CUT = cut_layers()
+
+
+def segments():
+    found = []
+    for plist, used in PIECES:
+        runs = []
+        for t, l, first, last, off in plist:
+            if t == len(TENSORS):
+                src, row, rows = t, 0, -(-last // 2) * 16
+            elif TENSORS[t][0] == "R":
+                src, row, rows = t, first * BLK * 8, (last - first) * BLK * 8
+            elif (t, l) in CUT:
+                c = TENSORS[t][1]
+                src, row, rows = len(TENSORS) + 1 + CUT.index((t, l)), first * c, (last - first) * c
+            else:
+                src, row, rows = t, l * BLK * TENSORS[t][1], BLK * TENSORS[t][1]
+            if runs and runs[-1][0] == src and runs[-1][1] + runs[-1][3] == row:
+                runs[-1][3] += rows
+            else:
+                runs.append([src, row, off * 8, rows])
+        end = runs[-1][2] + runs[-1][3]
+        if end < NR:
+            runs.append([0, 0, end, NR - end])
+        halves = ([], [])
+        for src, row, dst, rows in runs:
+            while rows > 0:
+                n = min(rows, CR - dst % CR)
+                d, k = divmod(dst // CR, NCH)
+                last = halves[d][-1] if halves[d] else None
+                if last and n == CR and last[0] == src and last[4] == CR and last[1] + last[5] * CR == row:
+                    last[5] += 1
+                else:
+                    halves[d].append([src, row, k, dst - d * (NR // 2), n, 1])
+                row, dst, rows = row + n, dst + n, rows - n
+        found.append(halves)
+    return found
+
+
+def rs_kernel(*refs):
+    count = len(TENSORS) + 1 + len(CUT)
+    srcs, (g_ref, sq_ref, r_ref, part, land, loads, outs, accum, sq_all,
+           send1, recv1, send2, recv2, load_sem, out_sem, sq_send, sq_recv) = refs[:count], refs[count:]
     me = lax.axis_index("dp")
     barrier_all(me)
     half = NR // 2
+    segs = segments()
+
+    def bits(d):
+        return 2 + 2 * d, 4 - 2 * d
+
+    def landing(d, q, slot, row, rows):
+        return r_ref.at[pl.ds(pl.multiple_of(((d * 2 + q) * 3 + slot) * half + row, 16), rows)]
 
     def hop(d, q, slot, k):
-        first, second = (2, 4) if d == 0 else (4, 2)
-        target = flip(me, 1) if slot == 0 else flip(me, first) if slot == 1 else flip(flip(me, first), 1)
-        owner = flip(target, second) if q == 0 else target
+        here = landing(d, q, slot, k * CR, CR)
         return pltpu.make_async_remote_copy(
-            src_ref=s_ref.at[pl.ds(owner * NR + d * half + k * CR, CR)],
-            dst_ref=r_ref.at[pl.ds(((d * 2 + q) * 3 + slot) * half + k * CR, CR)],
-            send_sem=send1.at[d, q, slot, k], recv_sem=recv1.at[d, q, slot, k],
-            device_id=(target,), device_id_type=MESH)
+            src_ref=here, dst_ref=here, send_sem=send1.at[d, q, slot, k], recv_sem=recv1.at[d, q, slot, k],
+            device_id=(flip(me, 1),), device_id_type=MESH)
 
     def pass_on(d, k):
-        second = 4 if d == 0 else 2
+        rows = pl.ds(pl.multiple_of(d * half + k * CR, 16), CR)
         return pltpu.make_async_remote_copy(
-            src_ref=part.at[pl.ds(d * half + k * CR, CR)], dst_ref=land.at[pl.ds(d * half + k * CR, CR)],
-            send_sem=send2.at[d, k], recv_sem=recv2.at[d, k],
-            device_id=(flip(me, second),), device_id_type=MESH)
-
-    for q in range(2):
-        @pl.loop(0, NCH)
-        def _(k):
-            for slot in (1, 2, 0):
-                for d in range(2):
-                    hop(d, q, slot, k).start()
-
-    def load(d, q, slot, k, buf):
-        second = 4 if d == 0 else 2
-        if slot == 3:
-            owner = flip(me, second) if q == 0 else me
-            src = s_ref.at[pl.ds(owner * NR + d * half + k * CR, CR)]
-        else:
-            src = r_ref.at[pl.ds(((d * 2 + q) * 3 + slot) * half + k * CR, CR)]
-        return pltpu.make_async_copy(src, loads.at[buf, slot], load_sem.at[buf, slot])
-
-    def fetch(d, q, k, buf):
+            src_ref=part.at[rows], dst_ref=land.at[rows], send_sem=send2.at[d, k], recv_sem=recv2.at[d, k],
+            device_id=(flip(me, bits(d)[1]),), device_id_type=MESH)
+
+    @pl.loop(0, 12)
+    def _(h):
+        q, turn, d = lax.div(h, 6), lax.rem(lax.div(h, 2), 3), lax.rem(h, 2)
+        slot = lax.rem(turn + 1, 3)
+        first, second = bits(d)
+        away = flip(me, first)
+        target = jnp.where(slot == 0, flip(me, 1), jnp.where(slot == 1, away, flip(away, 1)))
+        owner = jnp.where(q == 0, flip(target, second), target)
+        for r in range(DEV):
+            for dd in range(2):
+                @pl.when((owner == r) & (d == dd))
+                def _():
+                    for src, row, k0, dst, rows, chunks in segs[r][dd]:
+                        def send(i, carry, src=src, row=row, k0=k0, dst=dst, rows=rows):
+                            pltpu.make_async_remote_copy(
+                                src_ref=srcs[src].at[pl.ds(pl.multiple_of(row + i * CR, 8), rows)],
+                                dst_ref=r_ref.at[pl.ds(pl.multiple_of(
+                                    ((d * 2 + q) * 3 + slot) * half + dst + i * CR, 8), rows)],
+                                send_sem=send1.at[d, q, slot, k0 + i], recv_sem=recv1.at[d, q, slot, k0 + i],
+                                device_id=(target,), device_id_type=MESH).start()
+                            return carry
+                        if chunks == 1:
+                            send(0, 0)
+                        else:
+                            lax.fori_loop(0, chunks, send, 0)
+
+    def load(d, q, slot, k):
+        return pltpu.make_async_copy(landing(d, q, slot % 3, k * CR, CR), loads.at[d, slot], load_sem.at[d, slot])
+
+    def load_own(d, q, k):
+        owner = flip(me, bits(d)[1]) if q == 0 else me
+        for r in range(DEV):
+            @pl.when(owner == r)
+            def _(r=r):
+                for src, row, k0, dst, rows, chunks in segs[r][d]:
+                    inside = (k >= k0) & (k < k0 + chunks)
+                    at = row if chunks == 1 else pl.multiple_of(row + jnp.where(inside, k - k0, 0) * CR, 8)
+
+                    @pl.when(inside)
+                    def _(src=src, at=at, dst=dst, rows=rows):
+                        pltpu.make_async_copy(
+                            srcs[src].at[pl.ds(at, rows)],
+                            loads.at[d, 3, pl.ds(dst % CR, rows)], load_sem.at[d, 3]).start()
+
+    def fetch(d, q, k):
+        load_own(d, q, k)
         for slot in range(3):
             hop(d, q, slot, k).wait_recv()
+            load(d, q, slot, k).start()
+
+    def ready(d, q, k):
         for slot in range(4):
-            load(d, q, slot, k, buf).start()
-
-    def ready(d, q, k, buf):
-        for slot in range(4):
-            load(d, q, slot, k, buf).wait()
-
-    def total(buf, rows):
-        acc = loads[buf, 3, rows, :].astype(jnp.float32)
+            load(d, q, slot, k).wait()
+
+    def total(d, rows):
+        acc = loads[d, 3, rows, :].astype(jnp.float32)
         for slot in range(3):
-            acc = acc + loads[buf, slot, rows, :].astype(jnp.float32)
+            acc = acc + loads[d, slot, rows, :].astype(jnp.float32)
         return acc
 
     STEP = 112
+    accum[...] = jnp.zeros_like(accum)
+    used = functools.reduce(lambda acc, r: jnp.where(me == r, PIECES[r][1], acc), range(DEV), 0)
+
+    def out_copy(d, k):
+        return pltpu.make_async_copy(
+            outs.at[d], g_ref.at[pl.ds(pl.multiple_of(d * half + k * CR, 16), CR)], out_sem.at[d])
 
     for d in range(2):
-        fetch(d, 0, 0, d)
+        fetch(d, 0, jnp.int32(0))
 
     @pl.loop(0, NCH)
     def _(k):
         for d in range(2):
-            ready(d, 0, k, d)
+            ready(d, 0, k)
 
             @pl.loop(0, CR // STEP)
             def _(i):
-                rows = pl.ds(i * STEP, STEP)
-                part[pl.ds(d * half + k * CR + i * STEP, STEP), :] = total(d, rows)
+                rows = pl.ds(pl.multiple_of(i * STEP, 16), STEP)
+                part[pl.ds(pl.multiple_of(d * half + k * CR + i * STEP, 8), STEP), :] = total(d, rows)
 
             @pl.when(k + 1 < NCH)
             def _():
-                fetch(d, 0, k + 1, d)
+                fetch(d, 0, k + 1)
 
             pass_on(d, k).start()
 
-    accum[...] = jnp.zeros_like(accum)
-    skip_rows = me * 0
-
-    def out_copy(d, k):
-        return pltpu.make_async_copy(outs.at[d], g_ref.at[pl.ds(d * half + k * CR, CR)], out_sem.at[d])
-
     for d in range(2):
-        fetch(d, 1, 0, d)
+        fetch(d, 1, jnp.int32(0))
 
     @pl.loop(0, NCH)
     def _(k):
         for d in range(2):
-            ready(d, 1, k, d)
+            ready(d, 1, k)
             pass_on(d, k).wait_recv()
 
             @pl.when(k > 0)
@@ -181,20 +259,22 @@
 
             @pl.loop(0, CR // STEP)
             def _(i):
-                base = d * half + k * CR + i * STEP
-                g = (total(d, pl.ds(i * STEP, STEP)) + land[pl.ds(base, STEP), :]) * (1.0 / DEV)
-                outs[d, pl.ds(i * STEP, STEP), :] = g
+                base = pl.multiple_of(d * half + k * CR + i * STEP, 8)
+                rows = pl.ds(pl.multiple_of(i * STEP, 16), STEP)
+                g = (total(d, rows) + land[pl.ds(base, STEP), :]) * (1.0 / DEV)
+                outs[d, rows, :] = g
                 tile = lax.div(base, 8) + lax.broadcasted_iota(jnp.int32, (STEP // 8, 8, 128), 0)
                 g3 = g.reshape(STEP // 8, 8, 128)
-                accum[...] += jnp.sum(jnp.where(counted(me, tile), g3 * g3, 0.0), axis=0)
+                keep = counted(me, tile) & (tile < used)
+                accum[...] += jnp.sum(jnp.where(keep, g3 * g3, 0.0), axis=0)
 
             @pl.when(k + 1 < NCH)
             def _():
-                fetch(d, 1, k + 1, d)
+                fetch(d, 1, k + 1)
 
             out_copy(d, k).start()
 
-    sq_all[pl.ds(me * 8, 8), :] = accum[...]
+    sq_all[pl.ds(pl.multiple_of(me * 8, 8), 8), :] = accum[...]
     for d in range(2):
         out_copy(d, NCH - 1).wait()
     for d in range(2):
@@ -207,7 +287,7 @@
 
     def tell(step):
         return pltpu.make_async_remote_copy(
-            src_ref=accum, dst_ref=sq_all.at[pl.ds(me * 8, 8)],
+            src_ref=accum, dst_ref=sq_all.at[pl.ds(pl.multiple_of(me * 8, 8), 8)],
             send_sem=sq_send.at[step], recv_sem=sq_recv.at[step],
             device_id=(lax.rem(me + step + 1, DEV),), device_id_type=MESH)
 
@@ -227,28 +307,25 @@
         kind, tile, stride, row = UNITS[r][0]
         if row >= 0:
             continue
-        found.append((r, BLK, 1) if kind == "R" else (r, stride * kind // 8, stride))
+        found.append((r, BLK if kind == "R" else kind // 8))
     return found
 
 
 def counted(me, tile):
-    keep = tile >= 0
-    for r, tiles, period in shared_first():
-        skip = (tile < tiles) & (lax.rem(tile, period) == 0)
-        keep = keep & jnp.logical_not(skip & (me == r))
-    return keep
-
-
-def reduce_scatter(send):
+    first = functools.reduce(lambda acc, x: jnp.where(me == x[0], x[1], acc), shared_first(), 0)
+    return tile >= first
+
+
+def reduce_scatter(sources):
     half = NR // 2
     return pl.pallas_call(
         rs_kernel,
         name="reduce_scatter",
         out_shape=(jax.ShapeDtypeStruct((NR, 128), jnp.float32), jax.ShapeDtypeStruct((8, 128), jnp.float32),
                    jax.ShapeDtypeStruct((12 * half, 128), jnp.bfloat16)),
-        in_specs=[pl.BlockSpec(memory_space=pl.ANY)],
-        out_specs=(pl.BlockSpec(memory_space=pl.ANY), pl.BlockSpec(memory_space=pltpu.VMEM),
-                   pl.BlockSpec(memory_space=pl.ANY)),
+        in_specs=[pl.BlockSpec(memory_space=pltpu.HBM)] * len(sources),
+        out_specs=(pl.BlockSpec(memory_space=pltpu.HBM), pl.BlockSpec(memory_space=pltpu.VMEM),
+                   pl.BlockSpec(memory_space=pltpu.HBM)),
         scratch_shapes=[
             pltpu.VMEM((NR, 128), jnp.float32), pltpu.VMEM((NR, 128), jnp.float32),
             pltpu.VMEM((2, 4, CR, 128), jnp.bfloat16), pltpu.VMEM((2, CR, 128), jnp.float32),
@@ -258,7 +335,7 @@
             pltpu.SemaphoreType.DMA((2, 4)), pltpu.SemaphoreType.DMA((2,)),
             pltpu.SemaphoreType.DMA((DEV - 1,)), pltpu.SemaphoreType.DMA((DEV - 1,))],
         compiler_params=pltpu.CompilerParams(collective_id=0, has_side_effects=True, vmem_limit_bytes=60 << 20),
-    )(send)
+    )(*sources)
 
 
 BR = 1128
@@ -434,7 +511,7 @@
 
 def adam(scal, g, sq, m, v, p):
     block = pl.BlockSpec((BR, 128), lambda b, *_: (b, 0))
-    anywhere = pl.BlockSpec(memory_space=pl.ANY)
+    anywhere = pl.BlockSpec(memory_space=pltpu.HBM)
     flat_shape = jax.ShapeDtypeStruct((SROWS, 128), jnp.float32)
     return pl.pallas_call(
         adam_kernel,
@@ -507,7 +584,7 @@
 
 
 def all_gather(mine):
-    anywhere = pl.BlockSpec(memory_space=pl.ANY)
+    anywhere = pl.BlockSpec(memory_space=pltpu.HBM)
     return pl.pallas_call(
         ag_kernel,
         name="all_gather",
@@ -534,68 +611,160 @@
     return x.reshape(shape)
 
 
-def pack(views, tail):
-    parts = []
-    for plist, used in PIECES:
-        for t, l, first, last, _ in plist:
-            if t == len(TENSORS):
-                piece = tail
-            elif TENSORS[t][0] == "R":
-                piece = views[t][0, first:last]
-            else:
-                piece = views[t][l, :, first:last]
-            parts.append(piece.reshape(-1, 128))
-        if used < NT:
-            parts.append(jnp.zeros(((NT - used) * 8, 128), jnp.bfloat16))
-    return jnp.concatenate(parts, axis=0)
-
-
-def join(left, right, start, row_step, col_step, tile_step, lane_step, bound):
-    pos = start
-    for axis, step in enumerate((row_step, col_step, tile_step, lane_step)):
-        pos = pos + step * lax.broadcasted_iota(jnp.int32, left.shape, axis)
-    return jnp.where(pos < bound, left, right)
-
-
-def unpack(gathered, shapes):
-    outs = []
+def unpack_plan():
+    copies, shared, cuts = [], [], {}
     for t, (kind, rows, layers) in enumerate(TENSORS):
-        per_layer = {}
+        last_seen = None
         for r, (plist, _) in enumerate(PIECES):
             for pt, l, first, last, off in plist:
-                if pt == t:
-                    per_layer.setdefault(l, []).append((r, first, last, off))
-        done = []
-        for l in sorted(per_layer):
-            axis = 0 if kind == "R" else 1
-            parts = []
-            for r, first, last, off in per_layer[l]:
-                tiles = (last - first) * (BLK if kind == "R" else rows // 8)
-                base = (r * NT + off) * 8
-                shape = (last - first, BLK, 8, 128) if kind == "R" else (rows // 8, last - first, 8, 128)
-                piece = gathered[base:base + tiles * 8].reshape(shape)
-                if parts and first < parts[-1][2]:
-                    start = STARTS[t] + (first * 8 * D if kind == "R" else l * rows * D + first * 128 * rows)
-                    steps = (0, 128, D, 1) if kind == "R" else (8, 0, 1, rows)
-                    prev = parts.pop()
-                    size = prev[0].shape[axis]
-                    left = lax.slice_in_dim(prev[0], size - 1, size, axis=axis)
-                    right = lax.slice_in_dim(piece, 0, 1, axis=axis)
-                    if size > 1:
-                        parts.append((lax.slice_in_dim(prev[0], 0, size - 1, axis=axis), 0, 0))
-                    parts.append((join(left, right, start, *steps, r * SHARE), 0, 0))
-                    piece = lax.slice_in_dim(piece, 1, last - first, axis=axis)
-                parts.append((piece, first, last))
-            done.append(jnp.concatenate([p[0] for p in parts], axis=axis))
-        whole = jnp.stack(done)
-        if kind == "R":
-            whole = whole.reshape(1, rows // 8, BLK, 8, 128)
-        outs.append(from_tiles(t, whole, shapes[t]))
+                if pt != t:
+                    continue
+                src = r * NT + off
+                if (t, l) in CUT:
+                    cuts.setdefault((t, l), []).append((first, last, src, r * SHARE))
+                    continue
+                if kind == "C":
+                    copies.append([src, t, l * BLK * rows // 8, BLK * rows // 8])
+                    continue
+                begin = first
+                if last_seen and first < last_seen[0]:
+                    copies[-1][3] -= BLK
+                    shared.append((t, first, last_seen[1] - BLK, src, STARTS[t] + first * 8 * D, r * SHARE))
+                    begin = first + 1
+                copies.append([src + (begin - first) * BLK, t, begin * BLK, (last - begin) * BLK])
+                last_seen = (last, src + (last - first) * BLK)
+    pieces = []
+    for src, t, dst, tiles in copies:
+        while tiles > 0:
+            n = min(tiles, UN)
+            pieces.append((src, t, dst, n))
+            src, dst, tiles = src + n, dst + n, tiles - n
+    return pieces, shared, cuts
+
+
+UN = 480
+UBUF = 12
+
+
+def unpack_kernel(src_ref, *refs):
+    outs = refs[:len(TENSORS)]
+    ring, left, right, *layers, in_sem, out_sem, pair_sem, cut_sem = refs[len(TENSORS):]
+    pieces, shared, cuts = unpack_plan()
+
+    def take(i):
+        src, _, _, n = pieces[i]
+        return pltpu.make_async_copy(src_ref.at[pl.ds(src, n)], ring.at[i % UBUF, pl.ds(0, n)], in_sem.at[i % UBUF])
+
+    def give(i):
+        _, t, dst, n = pieces[i]
+        return pltpu.make_async_copy(ring.at[i % UBUF, pl.ds(0, n)], outs[t].at[pl.ds(dst, n)], out_sem.at[i % UBUF])
+
+    def pair(n):
+        _, _, a, b, _, _ = shared[n]
+        return (pltpu.make_async_copy(src_ref.at[pl.ds(a, BLK)], left.at[n], pair_sem.at[n, 0]),
+                pltpu.make_async_copy(src_ref.at[pl.ds(b, BLK)], right.at[n], pair_sem.at[n, 1]))
+
+    def cut_loads(n):
+        (t, _), sides = list(cuts.items())[n]
+        c8 = TENSORS[t][1] // 8
+        made = []
+        for side, (first, last, src, _) in enumerate(sides):
+            for j in range(first, last):
+                over = side == 1 and first < sides[0][1] and j == first
+                to = right.at[len(shared) + n, pl.ds(0, c8)] if over else layers[n].at[pl.ds(0, c8), j]
+                made.append(pltpu.make_async_copy(
+                    src_ref.at[pl.ds(src + (j - first) * c8, c8)], to, cut_sem.at[n, BLK if over else j]))
+        return made
+
+    def cut_stores(n):
+        (t, l), _ = list(cuts.items())[n]
+        c8 = TENSORS[t][1] // 8
+        return [pltpu.make_async_copy(layers[n].at[c], outs[t].at[pl.ds((l * c8 + c) * BLK, BLK)], cut_sem.at[n, c])
+                for c in range(c8)]
+
+    def spot(start, row_step, lane_step, tile_step, tiles):
+        shape = (tiles, 8, 128)
+        return (start + tile_step * lax.broadcasted_iota(jnp.int32, shape, 0)
+                + row_step * lax.broadcasted_iota(jnp.int32, shape, 1)
+                + lane_step * lax.broadcasted_iota(jnp.int32, shape, 2))
+
+    for n in range(len(shared)):
+        for c in pair(n):
+            c.start()
+    for n in range(len(cuts)):
+        for c in cut_loads(n):
+            c.start()
+    depth = UBUF // 2
+    for i in range(depth):
+        take(i).start()
+    for i in range(len(pieces)):
+        if i + depth < len(pieces):
+            if i + depth >= UBUF:
+                give(i + depth - UBUF).wait()
+            take(i + depth).start()
+        take(i).wait()
+        give(i).start()
+        if i == depth:
+            for n, (t, _, _, _, start, bound) in enumerate(shared):
+                for c in pair(n):
+                    c.wait()
+                keep = spot(start, D, 1, 128, BLK) < bound
+                left[n] = jnp.where(keep, left[n].astype(jnp.float32), right[n].astype(jnp.float32)).astype(jnp.bfloat16)
+            for n, ((t, l), sides) in enumerate(cuts.items()):
+                for c in cut_loads(n):
+                    c.wait()
+                rows = TENSORS[t][1]
+                j, bound = sides[1][0], sides[1][3]
+                if j < sides[0][1]:
+                    keep = spot(STARTS[t] + (l * D + j * 128) * rows, 1, rows, 8, rows // 8) < bound
+                    one = right[len(shared) + n, pl.ds(0, rows // 8)].astype(jnp.float32)
+                    here = pl.ds(0, rows // 8)
+                    layers[n][here, j] = jnp.where(keep, layers[n][here, j].astype(jnp.float32), one).astype(jnp.bfloat16)
+        if i == depth + 2:
+            for n, (t, g, _, _, _, _) in enumerate(shared):
+                pltpu.make_async_copy(left.at[n], outs[t].at[pl.ds(g * BLK, BLK)], pair_sem.at[n, 0]).start()
+            for n in range(len(cuts)):
+                for c in cut_stores(n):
+                    c.start()
+    for i in range(max(0, len(pieces) - UBUF), len(pieces)):
+        give(i).wait()
+    for n, (t, g, _, _, _, _) in enumerate(shared):
+        pltpu.make_async_copy(left.at[n], outs[t].at[pl.ds(g * BLK, BLK)], pair_sem.at[n, 0]).wait()
+    for n in range(len(cuts)):
+        for c in cut_stores(n):
+            c.wait()
+
+
+def unpack(gathered, shapes):
+    pieces, shared, cuts = unpack_plan()
+    anywhere = pl.BlockSpec(memory_space=pltpu.HBM)
+    tiles = pl.pallas_call(
+        unpack_kernel,
+        name="unpack",
+        out_shape=[jax.ShapeDtypeStruct((size // 1024, 8, 128), jnp.bfloat16) for size in SIZES],
+        in_specs=[anywhere], out_specs=[anywhere] * len(TENSORS),
+        scratch_shapes=[
+            pltpu.VMEM((UBUF, UN, 8, 128), jnp.bfloat16), pltpu.VMEM((len(shared) + 1, BLK, 8, 128), jnp.bfloat16),
+            pltpu.VMEM((len(shared) + len(cuts) + 1, BLK, 8, 128), jnp.bfloat16),
+            *[pltpu.VMEM((TENSORS[t][1] // 8 + 1, BLK, 8, 128), jnp.bfloat16) for t, _ in cuts],
+            pltpu.SemaphoreType.DMA((UBUF,)), pltpu.SemaphoreType.DMA((UBUF,)),
+            pltpu.SemaphoreType.DMA((len(shared), 2)), pltpu.SemaphoreType.DMA((len(cuts), BLK + 1))],
+        compiler_params=pltpu.CompilerParams(vmem_limit_bytes=48 << 20),
+    )(gathered.reshape(DEV * NT, 8, 128))
+    outs = [from_tiles(t, x.reshape(TENSORS[t][2], TENSORS[t][1] // 8, BLK, 8, 128), shapes[t])
+            for t, x in enumerate(tiles)]
     plist, _ = PIECES[DEV - 1]
-    off = plist[-1][4]
-    tail = gathered[((DEV - 1) * NT + off) * 8:((DEV - 1) * NT + off) * 8 + TAIL // 128].reshape(-1)
+    base = ((DEV - 1) * NT + plist[-1][4]) * 8
+    tail = gathered[base:base + TAIL // 128].reshape(-1)
     cut = math.prod(shapes[8])
     return outs + [tail[:cut].reshape(shapes[8]), tail[cut:].reshape(shapes[9])]
+
+
+def sources(grads):
+    views = [as_tiles(t, grads[t][0]) for t in range(len(TENSORS))]
+    tail = jnp.concatenate([grads[8].reshape(-1), grads[9].reshape(-1), jnp.zeros((-TAIL % 2048,), jnp.bfloat16)])
+    turned = [views[t][l].transpose(1, 0, 2, 3) for t, l in CUT]
+    return [x.reshape(-1, 128) for x in views + [tail] + turned]
 
 
 def solution(mesh):
@@ -603,9 +772,7 @@
         grads = arrays[:10]
         m, v, p, hyper = arrays[10:]
         shapes = [x.shape[1:] for x in grads]
-        views = [as_tiles(t, grads[t][0]) for t in range(8)]
-        tail = jnp.concatenate([grads[8].reshape(-1), grads[9].reshape(-1)])
-        share, squares, _ = reduce_scatter(pack(views, tail))
+        share, squares, _ = reduce_scatter(sources(grads))
         learn_rate, b1, b2, decay, max_norm = [hyper[i] for i in range(5)]
         scal = jnp.stack([learn_rate, b1, 1.0 - b1, b2, 1.0 - b2, 1.0 / (1.0 - b1 ** ADAM_STEP),
                           1.0 / (1.0 - b2 ** ADAM_STEP), decay, max_norm])

time: 1380 us -> 1230 us (0.89)
  local copies, waits for them, and re-layouts: 199 us -> 23.1 us
  Pallas kernels: 1160 us -> 1200 us
    unnamed x105 -> x7, local copies, waits for them, and re-layouts: 107 us -> 0.71 us
    slice x33 -> x3, local copies, waits for them, and re-layouts: 80.2 us -> 3.41 us  [sources(): turned = [views[t][l].transpose(1, 0, 2, 3) for t, l in CUT]]
    pallas_call x0 -> x1, Pallas kernels: none -> 48.8 us  [unpack(): pl.pallas_call(unpack_kernel, name='unpack', out_shape=[jax.ShapeDtypeStr...]
where the time goes in v2:
time: 1230 us
  Pallas kernels  1200 us (98%)
  local copies, waits for them, and re-layouts  23.1 us (2%)
    pallas_call x1, Pallas kernels, reduce_scatter(): pl.pallas_call(rs_kernel, name='reduce_scatter', out_shape=(jax.ShapeDtyp...  612 us
    pallas_call x1, Pallas kernels, all_gather(): pl.pallas_call(ag_kernel, name='all_gather', out_shape=jax.ShapeDtypeStru...  461 us
    pallas_call x1, Pallas kernels, adam(): pl.pallas_call(adam_kernel, name='adam', grid_spec=pltpu.PrefetchScalarGr...  79.6 us
    pallas_call x1, Pallas kernels, unpack(): pl.pallas_call(unpack_kernel, name='unpack', out_shape=[jax.ShapeDtypeStr...  48.8 us

profile of v2, /device:TPU:0, one launch (start us, length us, event | category | flops | bytes accessed | tf_op | source)
XLA Modules:
  0.0 1231.6 jit_solution(1086193568440894558)
XLA Ops:
  0.6 0.8 fusion
  1.4 1.3 fusion.1
  8.0 1.2 stack.19.scal
  9.3 0.7 copy.39
  10.0 1.0 reshape.176
  11.0 0.7 maximum_bitcast_fusion.refs_8_
  11.7 1.6 copy_bitcast_fusion.2
  13.3 0.7 slice.44
  14.0 0.0 slice-start
  14.0 8.0 copy_bitcast_fusion.1
  22.0 1.4 slice.45
  23.4 0.0 slice-done
  23.4 0.0 slice-done.1
  23.4 0.0 slice-done.2
  23.4 2.0 copy_bitcast_fusion
  25.4 1.4 slice.46
  26.7 612.0 %reduce_scatter.1 = (f32[36288,128]{1,0:T(8,128)}, f32[8,128]{1,0:T(8,128)}, bf16[217728,128]{1,0:T(8,128)(2,1)}) custom-call(bf16[122880,128]{1,0:T(8,128)(2,1)} %bitcast.158, bf16[11520,128]{1,0:T(8,128)(2,1)} %bitcast.166, bf16[5760,128]{1,0:T(8,128)(2,1)} %bitcast.168, bf16[5760,128]{1,0:T(8,128)(2,1)} %bitcast.165, bf16[11520,128]{1,0:T(8,128)(2,1)} %bitcast.167, ...), custom_call_target="tpu_custom_call" | custom-call | tf_op jit(solution)/shard_map/reduce_scatter/pallas_call | solution.py:321
  638.8 79.6 %adam.1 = (f32[35973,128]{1,0:T(8,128)}, f32[35973,128]{1,0:T(8,128)}, f32[35973,128]{1,0:T(8,128)}, bf16[290304,128]{1,0:T(8,128)(2,1)}) custom-call(s32[8,4455]{1,0:T(8,128)} %constant.8.clone.entry, s32[8,330]{1,0:T(8,128)} %constant.9.clone.span, f32[9]{0:T(128)} %stack.19.scal, f32[36288,128]{1,0:T(8,128)} %get-tuple-element.27.g_ref, ...), custom_call_target="tpu_custom_call" | custom-call | tf_op jit(solution)/shard_map/adam/pallas_call | solution.py:516
  718.4 461.4 %all_gather.1 = bf16[290304,128]{1,0:T(8,128)(2,1)} custom-call(bf16[290304,128]{1,0:T(8,128)(2,1)} %get-tuple-element.29.a_in), custom_call_target="tpu_custom_call", output_to_operand_aliasing={{}: (0, {})} | custom-call | tf_op jit(solution)/shard_map/all_gather/pallas_call | solution.py:588
  1179.8 0.7 slice.43
  1180.5 0.6 reshape.203
  1181.1 0.9 slice.42
  1182.1 0.7 reshape.202
  1182.8 48.8 %unpack.1 = (bf16[15360,8,128]{2,1,0:T(8,128)(2,1)}, bf16[1440,8,128]{2,1,0:T(8,128)(2,1)}, bf16[720,8,128]{2,1,0:T(8,128)(2,1)}, bf16[720,8,128]{2,1,0:T(8,128)...) custom-call(bf16[36288,8,128]{2,1,0:T(8,128)(2,1)} %bitcast.56.src_ref), custom_call_target="tpu_custom_call" | custom-call | tf_op jit(solution)/shard_map/unpack/pallas_call | solution.py:741
  (4 shorter events, 0.0 us)
Async XLA Ops:
  14.0 9.4 slice-start
  14.0 9.4 slice-start.1
  14.0 9.4 slice-start.2

commit v3 on v2

--- a/solution.py
+++ b/solution.py
@@ -10,10 +10,12 @@
 from jax.sharding import PartitionSpec as P
 
 ADAM_STEP = 7
+LN = 128
+SB = 8
 ADAM_EPS = 1e-8
 CLIP_EPS = 1e-6
 D = 3840
-BLK = D // 128
+BLK = D // LN
 LAYERS = 6
 DEV = 8
 TENSORS = (("R", 4096, 1), ("C", 64, LAYERS), ("C", 32, LAYERS), ("C", 32, LAYERS), ("R", 64 * LAYERS, 1),
@@ -24,9 +26,9 @@
 TAIL = LAYERS * 4 * D + LAYERS * 2 * 256
 TOTAL = DECAY + TAIL
 SHARE = TOTAL // DEV
-SROWS = SHARE // 128
+SROWS = SHARE // LN
 NT = 4536
-NR = NT * 8
+NR = NT * SB
 GUARD = 240
 NCH = 9
 CR = NR // 2 // NCH
@@ -43,10 +45,10 @@
                 a, b = max(lo, STARTS[t]), min(hi, STARTS[t] + SIZES[t])
                 if a >= b:
                     continue
-                g0, g1 = (a - STARTS[t]) // (8 * D), -((STARTS[t] - b) // (8 * D))
+                g0, g1 = (a - STARTS[t]) // (SB * D), -((STARTS[t] - b) // (SB * D))
                 plist.append((t, 0, g0, g1, off))
                 for g in range(g0, g1):
-                    ulist.append(("R", off + (g - g0) * BLK, 1, (STARTS[t] + g * 8 * D - lo) // 128))
+                    ulist.append(("R", off + (g - g0) * BLK, 1, (STARTS[t] + g * SB * D - lo) // LN))
                 off += (g1 - g0) * BLK
                 continue
             for l in range(layers):
@@ -54,16 +56,16 @@
                 a, b = max(lo, s), min(hi, s + rows * D)
                 if a >= b:
                     continue
-                j0, j1 = (a - s) // (128 * rows), -((s - b) // (128 * rows))
+                j0, j1 = (a - s) // (LN * rows), -((s - b) // (LN * rows))
                 plist.append((t, l, j0, j1, off))
                 whole = j1 - j0 == BLK
                 for j in range(j0, j1):
-                    at, stride = (j, BLK) if whole else ((j - j0) * (rows // 8), 1)
-                    ulist.append((rows, off + at, stride, (s + j * 128 * rows - lo) // 128))
-                off += (j1 - j0) * rows // 8
+                    at, stride = (j, BLK) if whole else ((j - j0) * (rows // SB), 1)
+                    ulist.append((rows, off + at, stride, (s + j * LN * rows - lo) // LN))
+                off += (j1 - j0) * rows // SB
         if hi > DECAY:
             for i in range(TAIL // 1024):
-                ulist.append(("T", off + i, 1, (DECAY - lo) // 128 + 8 * i))
+                ulist.append(("T", off + i, 1, (DECAY - lo) // LN + SB * i))
             plist.append((len(TENSORS), 0, 0, TAIL // 1024, off))
             off += TAIL // 1024
         assert off <= NT
@@ -102,7 +104,7 @@
             if t == len(TENSORS):
                 src, row, rows = t, 0, -(-last // 2) * 16
             elif TENSORS[t][0] == "R":
-                src, row, rows = t, first * BLK * 8, (last - first) * BLK * 8
+                src, row, rows = t, first * BLK * SB, (last - first) * BLK * SB
             elif (t, l) in CUT:
                 c = TENSORS[t][1]
                 src, row, rows = len(TENSORS) + 1 + CUT.index((t, l)), first * c, (last - first) * c
@@ -111,7 +113,7 @@
             if runs and runs[-1][0] == src and runs[-1][1] + runs[-1][3] == row:
                 runs[-1][3] += rows
             else:
-                runs.append([src, row, off * 8, rows])
+                runs.append([src, row, off * SB, rows])
         end = runs[-1][2] + runs[-1][3]
         if end < NR:
             runs.append([0, 0, end, NR - end])
@@ -172,9 +174,9 @@
                     for src, row, k0, dst, rows, chunks in segs[r][dd]:
                         def send(i, carry, src=src, row=row, k0=k0, dst=dst, rows=rows):
                             pltpu.make_async_remote_copy(
-                                src_ref=srcs[src].at[pl.ds(pl.multiple_of(row + i * CR, 8), rows)],
+                                src_ref=srcs[src].at[pl.ds(pl.multiple_of(row + i * CR, SB), rows)],
                                 dst_ref=r_ref.at[pl.ds(pl.multiple_of(
-                                    ((d * 2 + q) * 3 + slot) * half + dst + i * CR, 8), rows)],
+                                    ((d * 2 + q) * 3 + slot) * half + dst + i * CR, SB), rows)],
                                 send_sem=send1.at[d, q, slot, k0 + i], recv_sem=recv1.at[d, q, slot, k0 + i],
                                 device_id=(target,), device_id_type=MESH).start()
                             return carry
@@ -193,7 +195,7 @@
             def _(r=r):
                 for src, row, k0, dst, rows, chunks in segs[r][d]:
                     inside = (k >= k0) & (k < k0 + chunks)
-                    at = row if chunks == 1 else pl.multiple_of(row + jnp.where(inside, k - k0, 0) * CR, 8)
+                    at = row if chunks == 1 else pl.multiple_of(row + jnp.where(inside, k - k0, 0) * CR, SB)
 
                     @pl.when(inside)
                     def _(src=src, at=at, dst=dst, rows=rows):
@@ -236,7 +238,7 @@
             @pl.loop(0, CR // STEP)
             def _(i):
                 rows = pl.ds(pl.multiple_of(i * STEP, 16), STEP)
-                part[pl.ds(pl.multiple_of(d * half + k * CR + i * STEP, 8), STEP), :] = total(d, rows)
+                part[pl.ds(pl.multiple_of(d * half + k * CR + i * STEP, SB), STEP), :] = total(d, rows)
 
             @pl.when(k + 1 < NCH)
             def _():
@@ -259,12 +261,12 @@
 
             @pl.loop(0, CR // STEP)
             def _(i):
-                base = pl.multiple_of(d * half + k * CR + i * STEP, 8)
+                base = pl.multiple_of(d * half + k * CR + i * STEP, SB)
                 rows = pl.ds(pl.multiple_of(i * STEP, 16), STEP)
                 g = (total(d, rows) + land[pl.ds(base, STEP), :]) * (1.0 / DEV)
                 outs[d, rows, :] = g
-                tile = lax.div(base, 8) + lax.broadcasted_iota(jnp.int32, (STEP // 8, 8, 128), 0)
-                g3 = g.reshape(STEP // 8, 8, 128)
+                tile = lax.div(base, SB) + lax.broadcasted_iota(jnp.int32, (STEP // SB, SB, LN), 0)
+                g3 = g.reshape(STEP // SB, SB, LN)
                 keep = counted(me, tile) & (tile < used)
                 accum[...] += jnp.sum(jnp.where(keep, g3 * g3, 0.0), axis=0)
 
@@ -274,7 +276,7 @@
 
             out_copy(d, k).start()
 
-    sq_all[pl.ds(pl.multiple_of(me * 8, 8), 8), :] = accum[...]
+    sq_all[pl.ds(pl.multiple_of(me * SB, SB), SB), :] = accum[...]
     for d in range(2):
         out_copy(d, NCH - 1).wait()
     for d in range(2):
@@ -287,7 +289,7 @@
 
     def tell(step):
         return pltpu.make_async_remote_copy(
-            src_ref=accum, dst_ref=sq_all.at[pl.ds(pl.multiple_of(me * 8, 8), 8)],
+            src_ref=accum, dst_ref=sq_all.at[pl.ds(pl.multiple_of(me * SB, SB), SB)],
             send_sem=sq_send.at[step], recv_sem=sq_recv.at[step],
             device_id=(lax.rem(me + step + 1, DEV),), device_id_type=MESH)
 
@@ -295,10 +297,10 @@
         tell(step).start()
     for step in range(DEV - 1):
         tell(step).wait()
-    whole = sq_all[pl.ds(0, 8), :]
+    whole = sq_all[pl.ds(0, SB), :]
     for i in range(1, DEV):
-        whole = whole + sq_all[pl.ds(8 * i, 8), :]
-    sq_ref[...] = jnp.broadcast_to(jnp.sum(whole, keepdims=True), (8, 128))
+        whole = whole + sq_all[pl.ds(SB * i, SB), :]
+    sq_ref[...] = jnp.broadcast_to(jnp.sum(whole, keepdims=True), (SB, LN))
 
 
 def shared_first():
@@ -307,7 +309,7 @@
         kind, tile, stride, row = UNITS[r][0]
         if row >= 0:
             continue
-        found.append((r, BLK if kind == "R" else kind // 8))
+        found.append((r, BLK if kind == "R" else kind // SB))
     return found
 
 
@@ -321,15 +323,15 @@
     return pl.pallas_call(
         rs_kernel,
         name="reduce_scatter",
-        out_shape=(jax.ShapeDtypeStruct((NR, 128), jnp.float32), jax.ShapeDtypeStruct((8, 128), jnp.float32),
-                   jax.ShapeDtypeStruct((12 * half, 128), jnp.bfloat16)),
+        out_shape=(jax.ShapeDtypeStruct((NR, LN), jnp.float32), jax.ShapeDtypeStruct((SB, LN), jnp.float32),
+                   jax.ShapeDtypeStruct((12 * half, LN), jnp.bfloat16)),
         in_specs=[pl.BlockSpec(memory_space=pltpu.HBM)] * len(sources),
         out_specs=(pl.BlockSpec(memory_space=pltpu.HBM), pl.BlockSpec(memory_space=pltpu.VMEM),
                    pl.BlockSpec(memory_space=pltpu.HBM)),
         scratch_shapes=[
-            pltpu.VMEM((NR, 128), jnp.float32), pltpu.VMEM((NR, 128), jnp.float32),
-            pltpu.VMEM((2, 4, CR, 128), jnp.bfloat16), pltpu.VMEM((2, CR, 128), jnp.float32),
-            pltpu.VMEM((8, 128), jnp.float32), pltpu.VMEM((8 * DEV, 128), jnp.float32),
+            pltpu.VMEM((NR, LN), jnp.float32), pltpu.VMEM((NR, LN), jnp.float32),
+            pltpu.VMEM((2, 4, CR, LN), jnp.bfloat16), pltpu.VMEM((2, CR, LN), jnp.float32),
+            pltpu.VMEM((SB, LN), jnp.float32), pltpu.VMEM((SB * DEV, LN), jnp.float32),
             pltpu.SemaphoreType.DMA((2, 2, 3, NCH)), pltpu.SemaphoreType.DMA((2, 2, 3, NCH)),
             pltpu.SemaphoreType.DMA((2, NCH)), pltpu.SemaphoreType.DMA((2, NCH)),
             pltpu.SemaphoreType.DMA((2, 4)), pltpu.SemaphoreType.DMA((2,)),
@@ -338,24 +340,35 @@
     )(*sources)
 
 
-BR = 1128
+BR = 2304
 NB = -(-SROWS // BR)
-KINDS = ("R", 240, 64, 32, "T")
+STEP = 96
+KINDS = {"R": 1, 240: 3, 64: SB, 32: 16, "T": 1}
+PT = NT // NCH
 
 
 def unit_tables():
     depth = max(len([u for u in ulist if u[0] == kind]) for ulist in UNITS for kind in KINDS)
     entry = np.zeros((DEV, len(KINDS), 3, depth), np.int32)
-    span = np.zeros((DEV, len(KINDS), 2, NB + 1), np.int32)
+    span = np.zeros((DEV, len(KINDS) + 1, 2, NB + 1), np.int32)
+    blocks = range(NB)
     for r, ulist in enumerate(UNITS):
+        need, made = [NB - 1] * NCH, [0] * NCH
         for n, kind in enumerate(KINDS):
             mine = [u for u in ulist if u[0] == kind]
-            length = 8 if kind == "T" else 240 if kind == "R" else kind
+            length = SB if kind == "T" else GUARD if kind == "R" else kind
             for i, u in enumerate(mine):
-                entry[r, n, :, i] = (u[1] * 8, u[2] * 8, u[3] + GUARD)
-            for b in range(NB):
-                span[r, n, 0, b + 1] = sum(u[3] < (b + 1) * BR for u in mine)
-                span[r, n, 1, b + 1] = sum(u[3] + length <= (b + 1) * BR for u in mine) if b < NB - 1 else len(mine)
+                entry[r, n, :, i] = (u[1], u[2], u[3] + GUARD)
+                first = max(0, u[3] // BR)
+                last = min(NB - 1, (u[3] + length - 1) // BR)
+                count = 1 if kind == "T" else BLK if kind == "R" else kind // SB
+                for piece in {(u[1] + c * u[2]) // PT for c in range(count)}:
+                    need[piece] = min(need[piece], first)
+                    made[piece] = max(made[piece], last)
+            span[r, n, 0, 1:] = [sum(max(0, u[3] // BR) <= b for u in mine) for b in blocks]
+            span[r, n, 1, 1:] = [sum(min(NB - 1, (u[3] + length - 1) // BR) <= b for u in mine) for b in blocks]
+        span[r, -1, 0, 1:] = [sum(min(need[i:]) <= b for i in range(NCH)) for b in blocks]
+        span[r, -1, 1, 1:] = [sum(max(made[:i + 1]) <= b for i in range(NCH)) for b in blocks]
     return entry, span, depth
 
 
@@ -363,170 +376,188 @@
 
 
 def lanes(rows):
-    return lax.broadcasted_iota(jnp.int32, (rows, 128), 1)
+    return lax.broadcasted_iota(jnp.int32, (rows, LN), 1)
 
 
 def roll(x, shift):
-    shift = shift % 128
+    shift = shift % LN
     return x if shift == 0 else pltpu.roll(x, shift, 1)
 
 
-def to_flat(kind, tiles, flat, ta, tb, base, stride, row):
-    def tile(i):
-        return tiles[pl.ds(pl.multiple_of(base + i * stride, 8), 8), :]
-
-    if kind == "T":
-        flat[pl.ds(row, 8), :] = tile(0)
+def swap_blocks(xs, width):
+    per = len(xs)
+    lane = lanes(xs[0].shape[0])
+
+    def pick(choose):
+        out = choose(0)
+        for b in range(1, per):
+            out = jnp.where(lane >= b * width, choose(b), out)
+        return out
+
+    turned = [roll(pick(lambda b: xs[(b + t) % per]), t * width) for t in range(per)]
+    return [pick(lambda b: turned[(b - j) % per]) for j in range(per)]
+
+
+def to_flat(kind, units, tiles, flat, low, ta, tb):
+    del low
+    if kind == "T" or kind == "R":
+        for base, _, row in units:
+            if kind == "T":
+                flat[pl.ds(row, SB), :] = tiles[base]
+            else:
+                for c in range(BLK):
+                    flat[pl.ds(row + c, SB, stride=BLK), :] = tiles[base + c]
         return
-    if kind == "R":
-        for c in range(BLK):
-            flat[pl.ds(row + c, 8, stride=BLK), :] = tile(c)
+    if kind < LN:
+        per = LN // kind
+        sets = [units[i:i + per] for i in range(0, len(units), per)]
+        for n, some in enumerate(sets):
+            ta[n] = jnp.concatenate([tiles[base + i * stride] for base, stride, _ in some for i in range(kind // SB)]).T
+        for n, some in enumerate(sets):
+            for unit, x in zip(some, swap_blocks([ta[n, pl.ds(q, kind, stride=per), :] for q in range(per)], kind)):
+                flat[pl.ds(unit[-1], kind), :] = x
         return
-    count = kind // 8
-    grid = jnp.concatenate([tile(i) for i in range(min(count, 16))], axis=0)
-    if count < 16:
-        grid = jnp.concatenate([grid, jnp.zeros((128 - kind, 128), jnp.float32)], axis=0)
-    ta[...] = grid.T
-    if kind == 240:
-        grid = jnp.concatenate([tile(i) for i in range(16, 30)] + [jnp.zeros((16, 128), jnp.float32)], axis=0)
-        tb[...] = grid.T
-        lane = lanes(16)
-        for k in range(15):
-            r, o = divmod(128 * k, 240)
-            if o < 128:
-                x = ta[pl.ds(r, 16, stride=8), :]
-                if o > 0:
-                    x = jnp.where(lane >= o, x, tb[pl.ds(r, 16, stride=8), :])
+    for n, (base, stride, row) in enumerate(units):
+        ta[n] = jnp.concatenate([tiles[base + i * stride] for i in range(16)]).T
+        tb[n] = jnp.concatenate([tiles[base + i * stride] for i in range(16, BLK)] + [jnp.zeros((16, LN))]).T
+    lane = lanes(16)
+    for k in range(15):
+        r, o = divmod(LN * k, kind)
+        for n, (_, _, row) in enumerate(units):
+            x = (ta if o < LN else tb)[n, pl.ds(r, 16, stride=SB), :]
+            if 0 < o < LN:
+                x = jnp.where(lane >= o, x, tb[n, pl.ds(r, 16, stride=SB), :])
+            x = roll(x, -o)
+            if o + LN > kind:
+                x = jnp.where(lane >= kind - o, roll(ta[n, pl.ds(r + 1, 16, stride=SB), :], kind - o), x)
+            flat[pl.ds(row + k, 16, stride=15), :] = x
+
+
+def to_tiles(kind, units, tiles, flat, low, ta, tb):
+    del tiles
+
+    def put(at, value):
+        low[at] = value.astype(jnp.bfloat16)
+
+    if kind == "T" or kind == "R":
+        for base, _, row in units:
+            if kind == "T":
+                put(base, flat[pl.ds(row, SB), :])
             else:
-                x = tb[pl.ds(r, 16, stride=8), :]
-            x = roll(x, -o)
-            if o + 128 > 240:
-                x = jnp.where(lane >= 240 - o, roll(ta[pl.ds(r + 1, 16, stride=8), :], 240 - o), x)
-            flat[pl.ds(row + k, 16, stride=15), :] = x
+                for c in range(BLK):
+                    put(base + c, flat[pl.ds(row + c, SB, stride=BLK), :])
         return
-    per = 128 // kind
-    lane = lanes(kind)
-    x = ta[pl.ds(0, kind, stride=per), :]
-    for q in range(1, per):
-        x = jnp.where(lane >= q * kind, roll(ta[pl.ds(q, kind, stride=per), :], q * kind), x)
-    flat[pl.ds(row, kind), :] = x
-
-
-def to_tiles(kind, tiles, flat, ta, tb, base, stride, row):
-    def put(i, value):
-        tiles[pl.ds(pl.multiple_of(base + i * stride, 8), 8), :] = value
-
-    if kind == "T":
-        put(0, flat[pl.ds(row, 8), :])
+    if kind < LN:
+        per = LN // kind
+        sets = [units[i:i + per] for i in range(0, len(units), per)]
+        for n, some in enumerate(sets):
+            for q, x in enumerate(swap_blocks([flat[pl.ds(row, kind), :] for _, _, row in some], kind)):
+                ta[n, pl.ds(q, kind, stride=per), :] = x
+        for n, some in enumerate(sets):
+            grid = ta[n].T.reshape(16, SB, LN)
+            for u, (base, stride, _) in enumerate(some):
+                for i in range(kind // SB):
+                    put(base + i * stride, grid[u * (kind // SB) + i])
         return
-    if kind == "R":
-        for c in range(BLK):
-            put(c, flat[pl.ds(row + c, 8, stride=BLK), :])
-        return
-    if kind == 240:
-        lane = lanes(16)
-        for r in range(8):
-            k, o = divmod(240 * r, 128)
+    lane = lanes(16)
+    for r in range(SB):
+        k, o = divmod(kind * r, LN)
+        for n, (_, _, row) in enumerate(units):
             f = [flat[pl.ds(row + k + i, 16, stride=15), :] for i in range(3 if k + 2 < 15 else 2)]
-            first = f[0] if o == 0 else roll(jnp.where(lane >= o, f[0], f[1]), -o)
-            second = f[1] if o == 0 else roll(jnp.where(lane >= o, f[1], f[2]) if len(f) > 2 else f[1], -o)
-            ta[pl.ds(r, 16, stride=8), :] = first
-            tb[pl.ds(r, 16, stride=8), :] = second
-        grid = ta[...].T
-        for i in range(16):
-            put(i, grid[8 * i:8 * i + 8])
-        grid = tb[...].T
-        for i in range(14):
-            put(16 + i, grid[8 * i:8 * i + 8])
-        return
-    per = 128 // kind
-    f = flat[pl.ds(row, kind), :]
-    for q in range(per):
-        ta[pl.ds(q, kind, stride=per), :] = roll(f, -q * kind)
-    grid = ta[...].T
-    for i in range(kind // 8):
-        put(i, grid[8 * i:8 * i + 8])
+            ta[n, pl.ds(r, 16, stride=SB), :] = f[0] if o == 0 else roll(jnp.where(lane >= o, f[0], f[1]), -o)
+            tb[n, pl.ds(r, 16, stride=SB), :] = f[1] if o == 0 else roll(jnp.where(lane >= o, f[1], f[-1]), -o)
+    for n, (base, stride, _) in enumerate(units):
+        grid = jnp.concatenate([ta[n].T, tb[n].T]).reshape(32, SB, LN)
+        for i in range(BLK):
+            put(base + i * stride, grid[i])
 
 
 def adam_kernel(entry, span, scal, g_ref, sq_ref, m_ref, v_ref, p_ref, m_out, v_out, p_out, a_ref,
                 tiles, flat, ta, tb, low, g_sem, a_sem):
     me = lax.axis_index("dp")
     b = pl.program_id(0)
-    load = pltpu.make_async_copy(g_ref, tiles, g_sem)
+
+    def take(i):
+        here = pl.ds(i * PT, PT)
+        return pltpu.make_async_copy(g_ref.at[here], tiles.at[here], g_sem.at[i])
+
+    def give(i):
+        here = pl.ds(i * PT, PT)
+        return pltpu.make_async_copy(low.at[here], a_ref.at[pl.ds(me * NT + i * PT, PT)], a_sem.at[i])
+
+    def span_of(n, which, at):
+        return span[me, (n * 2 + which) * (NB + 1) + at]
 
     @pl.when(b == 0)
     def _():
-        load.start()
-        load.wait()
+        for i in range(NCH):
+            take(i).start()
+
+    pl.loop(span_of(len(KINDS), 0, b), span_of(len(KINDS), 0, b + 1))(lambda i: take(i).wait())
 
     def each(which, work):
-        for n, kind in enumerate(KINDS):
-            at = (n * 3) * DEPTH
-
-            def body(u, carry, kind=kind, at=at):
-                work(kind, tiles, flat, ta, tb, entry[me, at + u],
-                     entry[me, at + DEPTH + u], entry[me, at + 2 * DEPTH + u])
-                return carry
-
-            first = (n * 2 + which) * (NB + 1) + b
-            lax.fori_loop(span[me, first], span[me, first + 1], body, 0)
+        for n, (kind, group) in enumerate(KINDS.items()):
+            first, last = span_of(n, which, b), span_of(n, which, b + 1)
+            at = n * 3 * DEPTH
+
+            @pl.loop(0, lax.div(last - first + group - 1, group))
+            def _(t):
+                some = [jnp.minimum(first + t * group + x, last - 1) + at for x in range(group)]
+                work(kind, [(entry[me, u], entry[me, u + DEPTH], entry[me, u + 2 * DEPTH]) for u in some],
+                     tiles, flat, low, ta, tb)
 
     each(0, to_flat)
 
     learn_rate, b1, c1, b2, c2, i1, i2, decay, max_norm = [scal[i] for i in range(9)]
-    norm = jnp.sqrt(sq_ref[...])
-    clip = jnp.minimum(1.0, max_norm / (norm + CLIP_EPS))[0:1, :]
-    STEP = 24
+    clip = jnp.minimum(1.0, max_norm / (jnp.sqrt(sq_ref[...]) + CLIP_EPS))[:1]
 
     @pl.loop(0, BR // STEP)
     def _(i):
-        rows = pl.ds(i * STEP, STEP)
+        rows = pl.ds(pl.multiple_of(i * STEP, SB), STEP)
         local = b * BR + i * STEP
-        here = pl.ds(pl.multiple_of(GUARD + local, 8), STEP)
+        here = pl.ds(pl.multiple_of(GUARD + local, SB), STEP)
         h = flat[here, :] * clip
         m = b1 * m_ref[rows, :] + c1 * h
         v = b2 * v_ref[rows, :] + c2 * (h * h)
         p = p_ref[rows, :]
         m_out[rows, :] = m
         v_out[rows, :] = v
-        where = me * SROWS + local + lax.broadcasted_iota(jnp.int32, (STEP, 128), 0)
-        step = (m * i1) / (jnp.sqrt(v * i2) + ADAM_EPS) + jnp.where(where < DECAY // 128, decay * p, 0.0)
+        where = me * SROWS + local + lax.broadcasted_iota(jnp.int32, (STEP, LN), 0)
+        step = (m * i1) / (jnp.sqrt(v * i2) + ADAM_EPS) + jnp.where(where < DECAY // LN, decay * p, 0.0)
         p = p - learn_rate * step
         p_out[rows, :] = p
         flat[here, :] = p
 
+    pl.loop(span_of(len(KINDS), 1, jnp.maximum(b - 1, 0)), span_of(len(KINDS), 1, b))(lambda i: give(i).start())
     each(1, to_tiles)
 
     @pl.when(b == NB - 1)
     def _():
-        @pl.loop(0, NR // 96)
-        def _(i):
-            rows = pl.ds(pl.multiple_of(i * 96, 96), 96)
-            low[rows, :] = tiles[rows, :].astype(jnp.bfloat16)
-
-        put = pltpu.make_async_copy(low, a_ref.at[pl.ds(pl.multiple_of(me * NR, 16), NR)], a_sem)
-        put.start()
-        put.wait()
+        sent = span_of(len(KINDS), 1, NB - 1)
+        pl.loop(0, sent)(lambda i: give(i).wait())
+        pl.loop(sent, NCH)(lambda i: give(i).start())
+        pl.loop(sent, NCH)(lambda i: give(i).wait())
 
 
 def adam(scal, g, sq, m, v, p):
-    block = pl.BlockSpec((BR, 128), lambda b, *_: (b, 0))
+    block = pl.BlockSpec((BR, LN), lambda b, *_: (b, 0))
     anywhere = pl.BlockSpec(memory_space=pltpu.HBM)
-    flat_shape = jax.ShapeDtypeStruct((SROWS, 128), jnp.float32)
+    flat_shape = jax.ShapeDtypeStruct((SROWS, LN), jnp.float32)
+    turn = pltpu.VMEM((4, LN, LN), jnp.float32)
     return pl.pallas_call(
         adam_kernel,
         name="adam",
         grid_spec=pltpu.PrefetchScalarGridSpec(
             num_scalar_prefetch=3, grid=(NB,),
-            in_specs=[anywhere, pl.BlockSpec((8, 128), lambda b, *_: (0, 0)), block, block, block],
+            in_specs=[anywhere, pl.BlockSpec((SB, LN), lambda b, *_: (0, 0)), block, block, block],
             out_specs=[block, block, block, anywhere],
             scratch_shapes=[
-                pltpu.VMEM((NR, 128), jnp.float32), pltpu.VMEM((NB * BR + 2 * GUARD + 8, 128), jnp.float32),
-                pltpu.VMEM((128, 128), jnp.float32), pltpu.VMEM((128, 128), jnp.float32),
-                pltpu.VMEM((NR, 128), jnp.bfloat16), pltpu.SemaphoreType.DMA, pltpu.SemaphoreType.DMA]),
-        out_shape=[flat_shape, flat_shape, flat_shape, jax.ShapeDtypeStruct((DEV * NR, 128), jnp.bfloat16)],
+                pltpu.VMEM((NT, SB, LN), jnp.float32), pltpu.VMEM((NB * BR + 2 * GUARD + SB, LN), jnp.float32),
+                turn, turn, pltpu.VMEM((NT, SB, LN), jnp.bfloat16),
+                pltpu.SemaphoreType.DMA((NCH,)), pltpu.SemaphoreType.DMA((NCH,))]),
+        out_shape=[flat_shape, flat_shape, flat_shape, jax.ShapeDtypeStruct((DEV * NT, SB, LN), jnp.bfloat16)],
         compiler_params=pltpu.CompilerParams(dimension_semantics=("arbitrary",), vmem_limit_bytes=63 << 20),
-    )(jnp.asarray(ENTRY.reshape(DEV, -1)), jnp.asarray(SPAN.reshape(DEV, -1)), scal, g, sq, m, v, p)
+    )(jnp.asarray(ENTRY.reshape(DEV, -1)), jnp.asarray(SPAN.reshape(DEV, -1)), scal, g.reshape(NT, SB, LN), sq, m, v, p)
 
 
 def ag_kernel(a_in, a_ref, send, recv):
@@ -588,7 +619,7 @@
     return pl.pallas_call(
         ag_kernel,
         name="all_gather",
-        out_shape=jax.ShapeDtypeStruct((DEV * NR, 128), jnp.bfloat16),
+        out_shape=jax.ShapeDtypeStruct((DEV * NR, LN), jnp.bfloat16),
         in_specs=[anywhere], out_specs=anywhere,
         scratch_shapes=[pltpu.SemaphoreType.DMA((7, 2, NCH)), pltpu.SemaphoreType.DMA((7, 2, NCH))],
         input_output_aliases={0: 0},
@@ -600,7 +631,7 @@
     kind, rows, layers = TENSORS[t]
     if kind == "C":
         x = jnp.swapaxes(x, -1, -2)
-    return x.reshape(layers, rows // 8, 8, BLK, 128).transpose(0, 1, 3, 2, 4)
+    return x.reshape(layers, rows // SB, SB, BLK, LN).transpose(0, 1, 3, 2, 4)
 
 
 def from_tiles(t, x, shape):
@@ -624,12 +655,12 @@
                     cuts.setdefault((t, l), []).append((first, last, src, r * SHARE))
                     continue
                 if kind == "C":
-                    copies.append([src, t, l * BLK * rows // 8, BLK * rows // 8])
+                    copies.append([src, t, l * BLK * rows // SB, BLK * rows // SB])
                     continue
                 begin = first
                 if last_seen and first < last_seen[0]:
                     copies[-1][3] -= BLK
-                    shared.append((t, first, last_seen[1] - BLK, src, STARTS[t] + first * 8 * D, r * SHARE))
+                    shared.append((t, first, last_seen[1] - BLK, src, STARTS[t] + first * SB * D, r * SHARE))
                     begin = first + 1
                 copies.append([src + (begin - first) * BLK, t, begin * BLK, (last - begin) * BLK])
                 last_seen = (last, src + (last - first) * BLK)
@@ -666,7 +697,7 @@
 
     def cut_loads(n):
         (t, _), sides = list(cuts.items())[n]
-        c8 = TENSORS[t][1] // 8
+        c8 = TENSORS[t][1] // SB
         made = []
         for side, (first, last, src, _) in enumerate(sides):
             for j in range(first, last):
@@ -678,12 +709,12 @@
 
     def cut_stores(n):
         (t, l), _ = list(cuts.items())[n]
-        c8 = TENSORS[t][1] // 8
+        c8 = TENSORS[t][1] // SB
         return [pltpu.make_async_copy(layers[n].at[c], outs[t].at[pl.ds((l * c8 + c) * BLK, BLK)], cut_sem.at[n, c])
                 for c in range(c8)]
 
     def spot(start, row_step, lane_step, tile_step, tiles):
-        shape = (tiles, 8, 128)
+        shape = (tiles, SB, LN)
         return (start + tile_step * lax.broadcasted_iota(jnp.int32, shape, 0)
                 + row_step * lax.broadcasted_iota(jnp.int32, shape, 1)
                 + lane_step * lax.broadcasted_iota(jnp.int32, shape, 2))
@@ -708,7 +739,7 @@
             for n, (t, _, _, _, start, bound) in enumerate(shared):
                 for c in pair(n):
                     c.wait()
-                keep = spot(start, D, 1, 128, BLK) < bound
+                keep = spot(start, D, 1, LN, BLK) < bound
                 left[n] = jnp.where(keep, left[n].astype(jnp.float32), right[n].astype(jnp.float32)).astype(jnp.bfloat16)
             for n, ((t, l), sides) in enumerate(cuts.items()):
                 for c in cut_loads(n):
@@ -716,9 +747,9 @@
                 rows = TENSORS[t][1]
                 j, bound = sides[1][0], sides[1][3]
                 if j < sides[0][1]:
-                    keep = spot(STARTS[t] + (l * D + j * 128) * rows, 1, rows, 8, rows // 8) < bound
-                    one = right[len(shared) + n, pl.ds(0, rows // 8)].astype(jnp.float32)
-                    here = pl.ds(0, rows // 8)
+                    keep = spot(STARTS[t] + (l * D + j * LN) * rows, 1, rows, SB, rows // SB) < bound
+                    one = right[len(shared) + n, pl.ds(0, rows // SB)].astype(jnp.float32)
+                    here = pl.ds(0, rows // SB)
                     layers[n][here, j] = jnp.where(keep, layers[n][here, j].astype(jnp.float32), one).astype(jnp.bfloat16)
         if i == depth + 2:
             for n, (t, g, _, _, _, _) in enumerate(shared):
@@ -741,30 +772,33 @@
     tiles = pl.pallas_call(
         unpack_kernel,
         name="unpack",
-        out_shape=[jax.ShapeDtypeStruct((size // 1024, 8, 128), jnp.bfloat16) for size in SIZES],
+        out_shape=[jax.ShapeDtypeStruct((size // 1024, SB, LN), jnp.bfloat16) for size in SIZES],
         in_specs=[anywhere], out_specs=[anywhere] * len(TENSORS),
         scratch_shapes=[
-            pltpu.VMEM((UBUF, UN, 8, 128), jnp.bfloat16), pltpu.VMEM((len(shared) + 1, BLK, 8, 128), jnp.bfloat16),
-            pltpu.VMEM((len(shared) + len(cuts) + 1, BLK, 8, 128), jnp.bfloat16),
-            *[pltpu.VMEM((TENSORS[t][1] // 8 + 1, BLK, 8, 128), jnp.bfloat16) for t, _ in cuts],
+            pltpu.VMEM((UBUF, UN, SB, LN), jnp.bfloat16), pltpu.VMEM((len(shared) + 1, BLK, SB, LN), jnp.bfloat16),
+            pltpu.VMEM((len(shared) + len(cuts) + 1, BLK, SB, LN), jnp.bfloat16),
+            *[pltpu.VMEM((TENSORS[t][1] // SB + 1, BLK, SB, LN), jnp.bfloat16) for t, _ in cuts],
             pltpu.SemaphoreType.DMA((UBUF,)), pltpu.SemaphoreType.DMA((UBUF,)),
             pltpu.SemaphoreType.DMA((len(shared), 2)), pltpu.SemaphoreType.DMA((len(cuts), BLK + 1))],
         compiler_params=pltpu.CompilerParams(vmem_limit_bytes=48 << 20),
-    )(gathered.reshape(DEV * NT, 8, 128))
-    outs = [from_tiles(t, x.reshape(TENSORS[t][2], TENSORS[t][1] // 8, BLK, 8, 128), shapes[t])
+    )(gathered.reshape(DEV * NT, SB, LN))
+    outs = [from_tiles(t, x.reshape(TENSORS[t][2], TENSORS[t][1] // SB, BLK, SB, LN), shapes[t])
             for t, x in enumerate(tiles)]
     plist, _ = PIECES[DEV - 1]
-    base = ((DEV - 1) * NT + plist[-1][4]) * 8
-    tail = gathered[base:base + TAIL // 128].reshape(-1)
-    cut = math.prod(shapes[8])
-    return outs + [tail[:cut].reshape(shapes[8]), tail[cut:].reshape(shapes[9])]
+    base = ((DEV - 1) * NT + plist[-1][4]) * SB
+    tail = gathered[base:base + TAIL // LN].reshape(-1)
+    cut = math.prod(shapes[SB])
+    return outs + [tail[:cut].reshape(shapes[SB]), tail[cut:].reshape(shapes[9])]
 
 
 def sources(grads):
     views = [as_tiles(t, grads[t][0]) for t in range(len(TENSORS))]
-    tail = jnp.concatenate([grads[8].reshape(-1), grads[9].reshape(-1), jnp.zeros((-TAIL % 2048,), jnp.bfloat16)])
-    turned = [views[t][l].transpose(1, 0, 2, 3) for t, l in CUT]
-    return [x.reshape(-1, 128) for x in views + [tail] + turned]
+    tail = jnp.concatenate([grads[SB].reshape(-1), grads[9].reshape(-1), jnp.zeros((-TAIL % 2048,), jnp.bfloat16)])
+    turned = []
+    for t, l in CUT:
+        layer = jnp.swapaxes(lax.optimization_barrier(grads[t][:, l]), 1, 2)
+        turned.append(layer.reshape(-1, SB, BLK, LN).transpose(2, 0, 1, 3))
+    return [x.reshape(-1, LN) for x in views + [tail] + turned]
 
 
 def solution(mesh):
@@ -776,8 +810,8 @@
         learn_rate, b1, b2, decay, max_norm = [hyper[i] for i in range(5)]
         scal = jnp.stack([learn_rate, b1, 1.0 - b1, b2, 1.0 - b2, 1.0 / (1.0 - b1 ** ADAM_STEP),
                           1.0 / (1.0 - b2 ** ADAM_STEP), decay, max_norm])
-        m, v, p, mine = adam(scal, share, squares, *[x.reshape(SROWS, 128) for x in (m, v, p)])
-        params = unpack(all_gather(mine), shapes)
+        m, v, p, mine = adam(scal, share, squares, *[x.reshape(SROWS, LN) for x in (m, v, p)])
+        params = unpack(all_gather(mine.reshape(DEV * NR, LN)), shapes)
         return tuple(params) + tuple(x.reshape(SHARE) for x in (m, v, p))
 
     in_specs = tuple([P("dp")] * 10 + [P("dp"), P("dp"), P("dp"), P()])

time: 1230 us -> 1070 us (0.87)
  Pallas kernels: 1200 us -> 1050 us
    pallas_call x1, Pallas kernels: 461 us -> 326 us  [all_gather(): pl.pallas_call(ag_kernel, name='all_gather', out_shape=jax.ShapeDtypeStru...]
    pallas_call x1, Pallas kernels: 79.6 us -> 59.4 us  [adam(): pl.pallas_call(adam_kernel, name='adam', grid_spec=pltpu.PrefetchScalarGr...]
where the time goes in v3:
time: 1070 us
  Pallas kernels  1050 us (98%)
  local copies, waits for them, and re-layouts  16.1 us (2%)
    pallas_call x1, Pallas kernels, reduce_scatter(): pl.pallas_call(rs_kernel, name='reduce_scatter', out_shape=(jax.ShapeDtyp...  612 us
    pallas_call x1, Pallas kernels, all_gather(): pl.pallas_call(ag_kernel, name='all_gather', out_shape=jax.ShapeDtypeStru...  326 us
    pallas_call x1, Pallas kernels, adam(): pl.pallas_call(adam_kernel, name='adam', grid_spec=pltpu.PrefetchScalarGr...  59.4 us
    pallas_call x1, Pallas kernels, unpack(): pl.pallas_call(unpack_kernel, name='unpack', out_shape=[jax.ShapeDtypeStr...  48.8 us

profile of v3, /device:TPU:0, one launch (start us, length us, event | category | flops | bytes accessed | tf_op | source)
XLA Modules:
  0.0 1068.6 jit_solution(12772630339236700248)
XLA Ops:
  0.6 0.8 fusion
  1.4 1.3 fusion.1
  8.0 1.2 stack.19.scal
  9.3 0.7 copy.33
  10.0 1.0 reshape.191
  11.0 0.7 maximum_bitcast_fusion.refs_8_
  11.7 1.0 slice_bitcast_fusion.2
  12.6 0.7 copy.30
  13.4 1.6 slice_bitcast_fusion.1
  15.0 1.5 copy.31
  16.5 1.6 slice_bitcast_fusion
  18.2 1.5 copy.32
  19.7 612.0 %reduce_scatter.1 = (f32[36288,128]{1,0:T(8,128)}, f32[8,128]{1,0:T(8,128)}, bf16[217728,128]{1,0:T(8,128)(2,1)}) custom-call(bf16[122880,128]{1,0:T(8,128)(2,1)} %bitcast.153, bf16[11520,128]{1,0:T(8,128)(2,1)} %bitcast.165, bf16[5760,128]{1,0:T(8,128)(2,1)} %bitcast.168, bf16[5760,128]{1,0:T(8,128)(2,1)} %bitcast.167, bf16[11520,128]{1,0:T(8,128)(2,1)} %bitcast.166, ...), custom_call_target="tpu_custom_call" | custom-call | tf_op jit(solution)/shard_map/reduce_scatter/pallas_call | solution.py:323
  631.7 59.4 %adam.1 = (f32[35973,128]{1,0:T(8,128)}, f32[35973,128]{1,0:T(8,128)}, f32[35973,128]{1,0:T(8,128)}, bf16[36288,8,128]{2,1,0:T(8,128)(2,1)}) custom-call(s32[8,4455]{1,0:T(8,128)} %constant.8.clone.entry, s32[8,204]{1,0:T(8,128)} %constant.9.clone.span, f32[9]{0:T(128)} %stack.19.scal, f32[4536,8,128]{2,1,0:T(8,128)} %bitcast.154, ...), custom_call_target="tpu_custom_call" | custom-call | tf_op jit(solution)/shard_map/adam/pallas_call | solution.py:547
  691.2 325.6 %all_gather.1 = bf16[290304,128]{1,0:T(8,128)(2,1)} custom-call(bf16[290304,128]{1,0:T(8,128)(2,1)} %bitcast.60.a_in), custom_call_target="tpu_custom_call", output_to_operand_aliasing={{}: (0, {})} | custom-call | tf_op jit(solution)/shard_map/all_gather/pallas_call | solution.py:619
  1016.8 0.7 slice.43
  1017.5 0.6 reshape.223
  1018.1 0.9 slice.42
  1019.0 0.7 reshape.222
  1019.8 48.8 %unpack.1 = (bf16[15360,8,128]{2,1,0:T(8,128)(2,1)}, bf16[1440,8,128]{2,1,0:T(8,128)(2,1)}, bf16[720,8,128]{2,1,0:T(8,128)(2,1)}, bf16[720,8,128]{2,1,0:T(8,128)...) custom-call(bf16[36288,8,128]{2,1,0:T(8,128)(2,1)} %bitcast.61.src_ref), custom_call_target="tpu_custom_call" | custom-call | tf_op jit(solution)/shard_map/unpack/pallas_call | solution.py:772
  (1 shorter events, 0.0 us)

commit v4 on v3

--- a/solution.py
+++ b/solution.py
@@ -344,35 +344,51 @@
 NB = -(-SROWS // BR)
 STEP = 96
 KINDS = {"R": 1, 240: 3, 64: SB, 32: 16, "T": 1}
-PT = NT // NCH
-
-
-def unit_tables():
-    depth = max(len([u for u in ulist if u[0] == kind]) for ulist in UNITS for kind in KINDS)
-    entry = np.zeros((DEV, len(KINDS), 3, depth), np.int32)
-    span = np.zeros((DEV, len(KINDS) + 1, 2, NB + 1), np.int32)
-    blocks = range(NB)
+PIECES_OUT = 2 * NCH
+PT = NT // PIECES_OUT
+
+
+def unit_runs():
+    runs = {kind: [] for kind in KINDS}
+    need = np.full((PIECES_OUT, DEV), NB - 1)
+    made = np.zeros((PIECES_OUT, DEV), int)
     for r, ulist in enumerate(UNITS):
-        need, made = [NB - 1] * NCH, [0] * NCH
-        for n, kind in enumerate(KINDS):
+        for kind in KINDS:
             mine = [u for u in ulist if u[0] == kind]
-            length = SB if kind == "T" else GUARD if kind == "R" else kind
-            for i, u in enumerate(mine):
-                entry[r, n, :, i] = (u[1], u[2], u[3] + GUARD)
-                first = max(0, u[3] // BR)
-                last = min(NB - 1, (u[3] + length - 1) // BR)
-                count = 1 if kind == "T" else BLK if kind == "R" else kind // SB
-                for piece in {(u[1] + c * u[2]) // PT for c in range(count)}:
-                    need[piece] = min(need[piece], first)
-                    made[piece] = max(made[piece], last)
-            span[r, n, 0, 1:] = [sum(max(0, u[3] // BR) <= b for u in mine) for b in blocks]
-            span[r, n, 1, 1:] = [sum(min(NB - 1, (u[3] + length - 1) // BR) <= b for u in mine) for b in blocks]
-        span[r, -1, 0, 1:] = [sum(min(need[i:]) <= b for i in range(NCH)) for b in blocks]
-        span[r, -1, 1, 1:] = [sum(max(made[:i + 1]) <= b for i in range(NCH)) for b in blocks]
-    return entry, span, depth
-
-
-ENTRY, SPAN, DEPTH = unit_tables()
+            size, count = UNIT_SIZE[kind]
+            found = []
+            for i, (_, tile, stride, row) in enumerate(mine):
+                first = max(0, row // BR)
+                last = min(NB - 1, (row + size - 1) // BR)
+                for piece in {(tile + c * stride) // PT for c in range(count)}:
+                    need[piece, r] = min(need[piece, r], first)
+                    made[piece, r] = max(made[piece, r], last)
+                per = 1 if stride == BLK else count
+                if not found or stride != found[-1][-1] or row + GUARD != found[-1][2] + found[-1][0] * size:
+                    found.append([0, tile, row + GUARD, BLK * count, per, stride])
+                n, start, _, step, per, _ = found[-1]
+                assert tile == start + n // BLK * step + n % BLK * per
+                found[-1][0] += 1
+            for slot, run in enumerate(found):
+                if slot == len(runs[kind]):
+                    runs[kind].append(np.zeros((6, DEV), int))
+                runs[kind][slot][:, r] = run
+    for i in range(PIECES_OUT):
+        need[i] = need[i:].min(axis=0)
+        made[i] = made[:i + 1].max(axis=0)
+    return runs, need, made
+
+
+UNIT_SIZE = {"R": (GUARD, BLK), 240: (240, BLK), 64: (64, SB), 32: (32, 4), "T": (SB, 1)}
+RUNS, NEED, MADE = unit_runs()
+
+
+def by_owner(me, values):
+    out = int(values[0])
+    for r in range(1, DEV):
+        if int(values[r]) != int(values[r - 1]):
+            out = jnp.where(me >= r, int(values[r]), out)
+    return out
 
 
 def lanes(rows):
@@ -472,41 +488,72 @@
             put(base + i * stride, grid[i])
 
 
-def adam_kernel(entry, span, scal, g_ref, sq_ref, m_ref, v_ref, p_ref, m_out, v_out, p_out, a_ref,
-                tiles, flat, ta, tb, low, g_sem, a_sem):
+def step_kernel(scal, g_ref, sq_ref, m_ref, v_ref, p_ref, m_out, v_out, p_out, a_ref,
+                tiles, flat, ta, tb, low, g_sem, a_sem, send, recv):
     me = lax.axis_index("dp")
     b = pl.program_id(0)
+    xn, yn, pn = flip(me, 2), flip(me, 4), flip(me, 1)
+    diag = flip(xn, 4)
 
     def take(i):
         here = pl.ds(i * PT, PT)
         return pltpu.make_async_copy(g_ref.at[here], tiles.at[here], g_sem.at[i])
 
+    def keep(i):
+        return pltpu.make_async_copy(low.at[pl.ds(i * PT, PT)], a_ref.at[pl.ds(me * NT + i * PT, PT)], a_sem.at[i])
+
+    def copy(kind, d, k):
+        owner = (me, me, me, xn if d == 0 else yn, xn, yn, diag)[kind]
+        target = (xn, yn, pn, yn if d == 0 else xn, pn, pn, pn)[kind]
+        at = (2 * k + d) * PT
+        there = a_ref.at[pl.ds(owner * NT + at, PT)]
+        return pltpu.make_async_remote_copy(
+            src_ref=low.at[pl.ds(at, PT)] if kind < 3 else there, dst_ref=there,
+            send_sem=send.at[kind, d, k], recv_sem=recv.at[kind, d, k],
+            device_id=(target,), device_id_type=MESH)
+
     def give(i):
-        here = pl.ds(i * PT, PT)
-        return pltpu.make_async_copy(low.at[here], a_ref.at[pl.ds(me * NT + i * PT, PT)], a_sem.at[i])
-
-    def span_of(n, which, at):
-        return span[me, (n * 2 + which) * (NB + 1) + at]
+        for kind in range(3):
+            copy(kind, i % 2, i // 2).start()
+        keep(i).start()
 
     @pl.when(b == 0)
     def _():
-        for i in range(NCH):
+        barrier_all(me)
+        for i in range(PIECES_OUT):
             take(i).start()
 
-    pl.loop(span_of(len(KINDS), 0, b), span_of(len(KINDS), 0, b + 1))(lambda i: take(i).wait())
-
-    def each(which, work):
-        for n, (kind, group) in enumerate(KINDS.items()):
-            first, last = span_of(n, which, b), span_of(n, which, b + 1)
-            at = n * 3 * DEPTH
-
-            @pl.loop(0, lax.div(last - first + group - 1, group))
-            def _(t):
-                some = [jnp.minimum(first + t * group + x, last - 1) + at for x in range(group)]
-                work(kind, [(entry[me, u], entry[me, u + DEPTH], entry[me, u + 2 * DEPTH]) for u in some],
-                     tiles, flat, low, ta, tb)
-
-    each(0, to_flat)
+    made = [by_owner(me, MADE[i]) for i in range(PIECES_OUT)]
+    for i in range(PIECES_OUT):
+        pl.when(b == made[i] + 1)(functools.partial(give, i))
+    for i in range(PIECES_OUT):
+        pl.when(b == by_owner(me, NEED[i]))(lambda i=i: take(i).wait())
+
+    def upto(block, count, row, size, whole):
+        room = (block + 1) * BR + GUARD - row
+        n = lax.div(jnp.where(room > 0, room, 0) + (0 if whole else size - 1), size)
+        return jnp.where(n < count, n, count)
+
+    def each(whole, work):
+        for kind, group in KINDS.items():
+            size = UNIT_SIZE[kind][0]
+            for run in RUNS[kind]:
+                count, start, row, step, per, stride = [by_owner(me, x) for x in run]
+                first = jnp.where(b > 0, upto(b - 1, count, row, size, whole), 0)
+                last = upto(b, count, row, size, whole)
+                if whole:
+                    last = jnp.where(b < NB - 1, last, count)
+
+                @pl.loop(0, lax.div(last - first + group - 1, group))
+                def _(t):
+                    units = []
+                    for x in range(group):
+                        i = first + t * group + x
+                        i = jnp.where(i < last, i, last - 1)
+                        units.append((start + lax.div(i, BLK) * step + lax.rem(i, BLK) * per, stride, row + i * size))
+                    work(kind, units, tiles, flat, low, ta, tb)
+
+    each(False, to_flat)
 
     learn_rate, b1, c1, b2, c2, i1, i2, decay, max_norm = [scal[i] for i in range(9)]
     clip = jnp.minimum(1.0, max_norm / (jnp.sqrt(sq_ref[...]) + CLIP_EPS))[:1]
@@ -528,103 +575,63 @@
         p_out[rows, :] = p
         flat[here, :] = p
 
-    pl.loop(span_of(len(KINDS), 1, jnp.maximum(b - 1, 0)), span_of(len(KINDS), 1, b))(lambda i: give(i).start())
-    each(1, to_tiles)
+    each(True, to_tiles)
 
     @pl.when(b == NB - 1)
     def _():
-        sent = span_of(len(KINDS), 1, NB - 1)
-        pl.loop(0, sent)(lambda i: give(i).wait())
-        pl.loop(sent, NCH)(lambda i: give(i).start())
-        pl.loop(sent, NCH)(lambda i: give(i).wait())
-
-
-def adam(scal, g, sq, m, v, p):
+        for i in range(PIECES_OUT):
+            pl.when(made[i] == NB - 1)(functools.partial(give, i))
+
+        @pl.loop(0, NCH)
+        def _(k):
+            copy(0, 0, k).wait_recv()
+            copy(3, 0, k).start()
+            copy(4, 0, k).start()
+            copy(1, 1, k).wait_recv()
+            copy(3, 1, k).start()
+            copy(5, 1, k).start()
+            copy(0, 1, k).wait_recv()
+            copy(4, 1, k).start()
+            copy(1, 0, k).wait_recv()
+            copy(5, 0, k).start()
+
+        @pl.loop(0, NCH)
+        def _(k):
+            for d in range(2):
+                copy(3, d, k).wait_recv()
+                copy(6, d, k).start()
+
+        @pl.loop(0, NCH)
+        def _(k):
+            for d in range(2):
+                for kind in (2, 4, 5, 6):
+                    copy(kind, d, k).wait_recv()
+                for kind in range(7):
+                    copy(kind, d, k).wait_send()
+                keep(2 * k + d).wait()
+
+
+def step_and_gather(scal, g, sq, m, v, p):
     block = pl.BlockSpec((BR, LN), lambda b, *_: (b, 0))
     anywhere = pl.BlockSpec(memory_space=pltpu.HBM)
     flat_shape = jax.ShapeDtypeStruct((SROWS, LN), jnp.float32)
     turn = pltpu.VMEM((4, LN, LN), jnp.float32)
+    dma = pltpu.SemaphoreType.DMA
     return pl.pallas_call(
-        adam_kernel,
-        name="adam",
+        step_kernel,
+        name="step_and_gather",
         grid_spec=pltpu.PrefetchScalarGridSpec(
-            num_scalar_prefetch=3, grid=(NB,),
+            num_scalar_prefetch=1, grid=(NB,),
             in_specs=[anywhere, pl.BlockSpec((SB, LN), lambda b, *_: (0, 0)), block, block, block],
             out_specs=[block, block, block, anywhere],
             scratch_shapes=[
                 pltpu.VMEM((NT, SB, LN), jnp.float32), pltpu.VMEM((NB * BR + 2 * GUARD + SB, LN), jnp.float32),
                 turn, turn, pltpu.VMEM((NT, SB, LN), jnp.bfloat16),
-                pltpu.SemaphoreType.DMA((NCH,)), pltpu.SemaphoreType.DMA((NCH,))]),
+                dma((PIECES_OUT,)), dma((PIECES_OUT,)), dma((7, 2, NCH)), dma((7, 2, NCH))]),
         out_shape=[flat_shape, flat_shape, flat_shape, jax.ShapeDtypeStruct((DEV * NT, SB, LN), jnp.bfloat16)],
-        compiler_params=pltpu.CompilerParams(dimension_semantics=("arbitrary",), vmem_limit_bytes=63 << 20),
-    )(jnp.asarray(ENTRY.reshape(DEV, -1)), jnp.asarray(SPAN.reshape(DEV, -1)), scal, g.reshape(NT, SB, LN), sq, m, v, p)
-
-
-def ag_kernel(a_in, a_ref, send, recv):
-    del a_in
-    me = lax.axis_index("dp")
-    barrier_all(me)
-    half = NR // 2
-    xn, yn, pn = flip(me, 2), flip(me, 4), flip(me, 1)
-    diag = flip(xn, 4)
-
-    def copy(kind, d, k):
-        owner = (me, me, me, xn if d == 0 else yn, xn, yn, diag)[kind]
-        target = (xn, yn, pn, yn if d == 0 else xn, pn, pn, pn)[kind]
-        part = a_ref.at[pl.ds(owner * NR + d * half + k * CR, CR)]
-        return pltpu.make_async_remote_copy(
-            src_ref=part, dst_ref=part, send_sem=send.at[kind, d, k], recv_sem=recv.at[kind, d, k],
-            device_id=(target,), device_id_type=MESH)
-
-    for turn in range(2):
-        @pl.loop(0, NCH)
-        def _(k):
-            copy(0, turn, k).start()
-            copy(1, 1 - turn, k).start()
-            copy(2, turn, k).start()
-
-    @pl.loop(0, NCH)
-    def _(k):
-        copy(0, 0, k).wait_recv()
-        copy(3, 0, k).start()
-        copy(4, 0, k).start()
-        copy(1, 1, k).wait_recv()
-        copy(3, 1, k).start()
-        copy(5, 1, k).start()
-
-    @pl.loop(0, NCH)
-    def _(k):
-        copy(0, 1, k).wait_recv()
-        copy(4, 1, k).start()
-        copy(1, 0, k).wait_recv()
-        copy(5, 0, k).start()
-
-    @pl.loop(0, NCH)
-    def _(k):
-        for d in range(2):
-            copy(3, d, k).wait_recv()
-            copy(6, d, k).start()
-
-    @pl.loop(0, NCH)
-    def _(k):
-        for d in range(2):
-            for kind in (2, 4, 5, 6):
-                copy(kind, d, k).wait_recv()
-            for kind in range(7):
-                copy(kind, d, k).wait_send()
-
-
-def all_gather(mine):
-    anywhere = pl.BlockSpec(memory_space=pltpu.HBM)
-    return pl.pallas_call(
-        ag_kernel,
-        name="all_gather",
-        out_shape=jax.ShapeDtypeStruct((DEV * NR, LN), jnp.bfloat16),
-        in_specs=[anywhere], out_specs=anywhere,
-        scratch_shapes=[pltpu.SemaphoreType.DMA((7, 2, NCH)), pltpu.SemaphoreType.DMA((7, 2, NCH))],
-        input_output_aliases={0: 0},
-        compiler_params=pltpu.CompilerParams(collective_id=1, has_side_effects=True),
-    )(mine)
+        compiler_params=pltpu.CompilerParams(
+            dimension_semantics=("arbitrary",), vmem_limit_bytes=63 << 20, collective_id=1, has_side_effects=True),
+    )(scal, g.reshape(NT, SB, LN), sq, m, v, p)
 
 
 def as_tiles(t, x):
@@ -810,8 +817,8 @@
         learn_rate, b1, b2, decay, max_norm = [hyper[i] for i in range(5)]
         scal = jnp.stack([learn_rate, b1, 1.0 - b1, b2, 1.0 - b2, 1.0 / (1.0 - b1 ** ADAM_STEP),
                           1.0 / (1.0 - b2 ** ADAM_STEP), decay, max_norm])
-        m, v, p, mine = adam(scal, share, squares, *[x.reshape(SROWS, LN) for x in (m, v, p)])
-        params = unpack(all_gather(mine.reshape(DEV * NR, LN)), shapes)
+        m, v, p, gathered = step_and_gather(scal, share, squares, *[x.reshape(SROWS, LN) for x in (m, v, p)])
+        params = unpack(gathered.reshape(DEV * NR, LN), shapes)
         return tuple(params) + tuple(x.reshape(SHARE) for x in (m, v, p))
 
     in_specs = tuple([P("dp")] * 10 + [P("dp"), P("dp"), P("dp"), P()])

time: 1070 us -> 1040 us (0.972)
  Pallas kernels: 1050 us -> 978 us
  local copies, waits for them, and re-layouts: 16.1 us -> 52.7 us
    pallas_call x2 -> x1, Pallas kernels: 385 us -> 318 us  [step_and_gather(): pl.pallas_call(step_kernel, name='step_and_gather', grid_spec=pltpu.Prefe...]
    unnamed x1 -> x16, local copies, waits for them, and re-layouts: 0.7 us -> 37.4 us
where the time goes in v4:
time: 1040 us
  Pallas kernels  978 us (94%)
  local copies, waits for them, and re-layouts  52.7 us (5%)
    pallas_call x1, Pallas kernels, reduce_scatter(): pl.pallas_call(rs_kernel, name='reduce_scatter', out_shape=(jax.ShapeDtyp...  612 us
    pallas_call x1, Pallas kernels, step_and_gather(): pl.pallas_call(step_kernel, name='step_and_gather', grid_spec=pltpu.Prefe...  318 us
    pallas_call x1, Pallas kernels, unpack(): pl.pallas_call(unpack_kernel, name='unpack', out_shape=[jax.ShapeDtypeStr...  48.7 us
    unnamed x16, local copies, waits for them, and re-layouts  37.4 us

profile of v4, /device:TPU:0, one launch (start us, length us, event | category | flops | bytes accessed | tf_op | source)
XLA Modules:
  0.0 1037.7 jit_solution(14644019609625388348)
XLA Ops:
  0.6 0.8 fusion
  1.4 1.3 fusion.1
  8.0 1.2 stack.19.scal
  9.3 0.7 copy.30
  10.0 1.0 reshape.188
  11.0 0.7 maximum_bitcast_fusion.refs_8_
  11.7 1.0 slice_bitcast_fusion.2
  12.6 0.7 copy.27
  13.4 1.6 slice_bitcast_fusion.1
  15.0 1.5 copy.28
  16.5 1.6 slice_bitcast_fusion
  18.2 1.5 copy.29
  19.7 612.1 %reduce_scatter.1 = (f32[36288,128]{1,0:T(8,128)}, f32[8,128]{1,0:T(8,128)}, bf16[217728,128]{1,0:T(8,128)(2,1)}) custom-call(bf16[122880,128]{1,0:T(8,128)(2,1)} %bitcast.151, bf16[11520,128]{1,0:T(8,128)(2,1)} %bitcast.168, bf16[5760,128]{1,0:T(8,128)(2,1)} %bitcast.171, bf16[5760,128]{1,0:T(8,128)(2,1)} %bitcast.170, bf16[11520,128]{1,0:T(8,128)(2,1)} %bitcast.169, ...), custom_call_target="tpu_custom_call" | custom-call | tf_op jit(solution)/shard_map/reduce_scatter/pallas_call | solution.py:323
  631.8 317.6 %step_and_gather.1 = (f32[35973,128]{1,0:T(8,128)}, f32[35973,128]{1,0:T(8,128)}, f32[35973,128]{1,0:T(8,128)}, bf16[36288,8,128]{2,1,0:T(8,128)(2,1)}) custom-call(f32[9]{0:T(128)} %stack.19.scal, f32[4536,8,128]{2,1,0:T(8,128)} %bitcast.152, f32[8,128]{1,0:T(8,128)} %get-tuple-element.28.sq_ref, f32[35973,128]{1,0:T(8,128)} %bitcast.153, ...), custom_call_target="tpu_custom_call" | custom-call | tf_op jit(solution)/shard_map/step_and_gather/pallas_call | solution.py:620
  949.4 0.7 slice.44
  950.0 0.6 reshape.218
  950.7 0.9 slice.43
  951.6 48.7 %unpack.1 = (bf16[15360,8,128]{2,1,0:T(8,128)(2,1)}, bf16[1440,8,128]{2,1,0:T(8,128)(2,1)}, bf16[720,8,128]{2,1,0:T(8,128)(2,1)}, bf16[720,8,128]{2,1,0:T(8,128)...) custom-call(bf16[36288,8,128]{2,1,0:T(8,128)(2,1)} %get-tuple-elemen, ...), custom_call_target="tpu_custom_call" | custom-call | tf_op jit(solution)/shard_map/unpack/pallas_call | solution.py:779
  1000.3 0.7 reshape.217
  1001.0 16.2 %copy.34 = f32[4604544]{0:T(1024)} copy(f32[4604544]{0:T(1024)} %bitcast.160) | data formatting | bytes 36836352
  1017.2 2.0 copy-done
  1019.2 9.2 copy.35
  1028.5 2.1 slice-done.3
  1031.0 6.7 copy.36
  (12 shorter events, 0.4 us)
Async XLA Ops:
  1001.0 18.2 %copy-start = (f32[35973,128]{1,0:T(8,128)S(1)}, f32[35973,128]{1,0:T(8,128)}, u32[]{:S(2)}) copy-start(f32[35973,128]{1,0:T(8,128)} %get-tuple-element.39) | copy-start | bytes 55254532
  1001.0 27.4 %slice-start = ((s8[18419712]{0:T(1024)(128)(4,1)}), s8[4194304]{0:T(1024)(128)(4,1)S(1)}, s32[]{:S(2)}) async-start(s8[18419712]{0:T(1024)(128)(4,1)} %bitcast.156), calls=%async_computation | async-start | bytes 8388608
  1001.0 27.4 %slice-start.1 = ((s8[18419712]{0:T(1024)(128)(4,1)}), s8[4194304]{0:T(1024)(128)(4,1)S(1)}, s32[]{:S(2)}) async-start(s8[18419712]{0:T(1024)(128)(4,1)} %bitcast.156), calls=%async_computation.1 | async-start | bytes 8388608
  1001.0 27.4 %slice-start.2 = ((s8[18419712]{0:T(1024)(128)(4,1)}), s8[4194304]{0:T(1024)(128)(4,1)S(1)}, s32[]{:S(2)}) async-start(s8[18419712]{0:T(1024)(128)(4,1)} %bitcast.156), calls=%async_computation.2 | async-start | bytes 8388608
  1019.2 11.4 %slice-start.3 = ((s8[18419712]{0:T(1024)(128)(4,1)}), s8[4194304]{0:T(1024)(128)(4,1)S(1)}, s32[]{:S(2)}) async-start(s8[18419712]{0:T(1024)(128)(4,1)} %bitcast.156), calls=%async_computation.3 | async-start | bytes 8388608
  1019.2 11.8 %slice-start.4 = ((s8[18419712]{0:T(1024)(128)(4,1)}), s8[1642496]{0:T(1024)(128)(4,1)S(1)}, s32[]{:S(2)}) async-start(s8[18419712]{0:T(1024)(128)(4,1)} %bitcast.156), calls=%async_computation.4 | async-start | bytes 3284992

commit v5 on v4

--- a/solution.py
+++ b/solution.py
@@ -340,11 +340,12 @@
     )(*sources)
 
 
-BR = 2304
+BR = 1152
 NB = -(-SROWS // BR)
 STEP = 96
 KINDS = {"R": 1, 240: 3, 64: SB, 32: 16, "T": 1}
-PIECES_OUT = 2 * NCH
+ACH = 18
+PIECES_OUT = 2 * ACH
 PT = NT // PIECES_OUT
 
 
@@ -520,9 +521,9 @@
     @pl.when(b == 0)
     def _():
         barrier_all(me)
-        for i in range(PIECES_OUT):
-            take(i).start()
-
+
+    for i in range(PIECES_OUT):
+        pl.when(b == by_owner(me, np.maximum(NEED[i] - 3, 0)))(lambda i=i: take(i).start())
     made = [by_owner(me, MADE[i]) for i in range(PIECES_OUT)]
     for i in range(PIECES_OUT):
         pl.when(b == made[i] + 1)(functools.partial(give, i))
@@ -555,7 +556,13 @@
 
     each(False, to_flat)
 
-    learn_rate, b1, c1, b2, c2, i1, i2, decay, max_norm = [scal[i] for i in range(9)]
+    learn_rate, b1, b2, decay, max_norm = [scal[i] for i in range(5)]
+    c1, c2 = 1.0 - b1, 1.0 - b2
+
+    def correction(beta):
+        return 1.0 / (1.0 - jnp.full((1, LN), beta) ** ADAM_STEP)
+
+    i1, i2 = correction(b1), correction(b2)
     clip = jnp.minimum(1.0, max_norm / (jnp.sqrt(sq_ref[...]) + CLIP_EPS))[:1]
 
     @pl.loop(0, BR // STEP)
@@ -582,7 +589,7 @@
         for i in range(PIECES_OUT):
             pl.when(made[i] == NB - 1)(functools.partial(give, i))
 
-        @pl.loop(0, NCH)
+        @pl.loop(0, ACH)
         def _(k):
             copy(0, 0, k).wait_recv()
             copy(3, 0, k).start()
@@ -595,13 +602,13 @@
             copy(1, 0, k).wait_recv()
             copy(5, 0, k).start()
 
-        @pl.loop(0, NCH)
+        @pl.loop(0, ACH)
         def _(k):
             for d in range(2):
                 copy(3, d, k).wait_recv()
                 copy(6, d, k).start()
 
-        @pl.loop(0, NCH)
+        @pl.loop(0, ACH)
         def _(k):
             for d in range(2):
                 for kind in (2, 4, 5, 6):
@@ -627,7 +634,7 @@
             scratch_shapes=[
                 pltpu.VMEM((NT, SB, LN), jnp.float32), pltpu.VMEM((NB * BR + 2 * GUARD + SB, LN), jnp.float32),
                 turn, turn, pltpu.VMEM((NT, SB, LN), jnp.bfloat16),
-                dma((PIECES_OUT,)), dma((PIECES_OUT,)), dma((7, 2, NCH)), dma((7, 2, NCH))]),
+                dma((PIECES_OUT,)), dma((PIECES_OUT,)), dma((7, 2, ACH)), dma((7, 2, ACH))]),
         out_shape=[flat_shape, flat_shape, flat_shape, jax.ShapeDtypeStruct((DEV * NT, SB, LN), jnp.bfloat16)],
         compiler_params=pltpu.CompilerParams(
             dimension_semantics=("arbitrary",), vmem_limit_bytes=63 << 20, collective_id=1, has_side_effects=True),
@@ -798,14 +805,46 @@
     return outs + [tail[:cut].reshape(shapes[SB]), tail[cut:].reshape(shapes[9])]
 
 
+def turn_kernel(*refs):
+    count = len(CUT)
+    srcs, outs, bufs, sems, done = refs[:count], refs[count:2 * count], refs[2 * count:3 * count], *refs[3 * count:]
+
+    def take(n, c):
+        t, l = CUT[n]
+        c8 = TENSORS[t][1] // SB
+        return pltpu.make_async_copy(srcs[n].at[pl.ds((l * c8 + c) * BLK, BLK)], bufs[n].at[:, c], sems.at[n, c])
+
+    def give(n):
+        return pltpu.make_async_copy(bufs[n], outs[n], done.at[n])
+
+    every = [(n, c) for n, (t, _) in enumerate(CUT) for c in range(TENSORS[t][1] // SB)]
+    for n, c in every:
+        take(n, c).start()
+    for n, c in every:
+        take(n, c).wait()
+        if (n, c + 1) not in every:
+            give(n).start()
+    for n in range(count):
+        give(n).wait()
+
+
+def turn(views):
+    shapes = [(BLK, TENSORS[t][1] // SB, SB, LN) for t, _ in CUT]
+    anywhere = pl.BlockSpec(memory_space=pltpu.HBM)
+    return pl.pallas_call(
+        turn_kernel,
+        name="turn",
+        out_shape=[jax.ShapeDtypeStruct(x, jnp.bfloat16) for x in shapes],
+        in_specs=[anywhere] * len(CUT), out_specs=[anywhere] * len(CUT),
+        scratch_shapes=[pltpu.VMEM(x, jnp.bfloat16) for x in shapes]
+        + [pltpu.SemaphoreType.DMA((len(CUT), BLK)), pltpu.SemaphoreType.DMA((len(CUT),))],
+    )(*[views[t].reshape(-1, SB, LN) for t, _ in CUT])
+
+
 def sources(grads):
     views = [as_tiles(t, grads[t][0]) for t in range(len(TENSORS))]
     tail = jnp.concatenate([grads[SB].reshape(-1), grads[9].reshape(-1), jnp.zeros((-TAIL % 2048,), jnp.bfloat16)])
-    turned = []
-    for t, l in CUT:
-        layer = jnp.swapaxes(lax.optimization_barrier(grads[t][:, l]), 1, 2)
-        turned.append(layer.reshape(-1, SB, BLK, LN).transpose(2, 0, 1, 3))
-    return [x.reshape(-1, LN) for x in views + [tail] + turned]
+    return [x.reshape(-1, LN) for x in [*views, tail, *turn(views)]]
 
 
 def solution(mesh):
@@ -814,10 +853,7 @@
         m, v, p, hyper = arrays[10:]
         shapes = [x.shape[1:] for x in grads]
         share, squares, _ = reduce_scatter(sources(grads))
-        learn_rate, b1, b2, decay, max_norm = [hyper[i] for i in range(5)]
-        scal = jnp.stack([learn_rate, b1, 1.0 - b1, b2, 1.0 - b2, 1.0 / (1.0 - b1 ** ADAM_STEP),
-                          1.0 / (1.0 - b2 ** ADAM_STEP), decay, max_norm])
-        m, v, p, gathered = step_and_gather(scal, share, squares, *[x.reshape(SROWS, LN) for x in (m, v, p)])
+        m, v, p, gathered = step_and_gather(hyper, share, squares, *[x.reshape(SROWS, LN) for x in (m, v, p)])
         params = unpack(gathered.reshape(DEV * NR, LN), shapes)
         return tuple(params) + tuple(x.reshape(SHARE) for x in (m, v, p))
 

time: 1040 us -> 1030 us (level)
  local copies, waits for them, and re-layouts: 52.7 us -> 41.3 us
where the time goes in v5:
time: 1030 us; the launch traced here: 1020 us
  Pallas kernels  981 us (95%)
  local copies, waits for them, and re-layouts  41.3 us (4%)
    pallas_call x1, Pallas kernels, reduce_scatter(): pl.pallas_call(rs_kernel, name='reduce_scatter', out_shape=(jax.ShapeDtyp...  612 us
    pallas_call x1, Pallas kernels, step_and_gather(): pl.pallas_call(step_kernel, name='step_and_gather', grid_spec=pltpu.Prefe...  316 us
    pallas_call x1, Pallas kernels, unpack(): pl.pallas_call(unpack_kernel, name='unpack', out_shape=[jax.ShapeDtypeStr...  48.7 us
    unnamed x16, local copies, waits for them, and re-layouts  37.4 us

profile of v5, /device:TPU:0, one launch (start us, length us, event | category | flops | bytes accessed | tf_op | source)
XLA Modules:
  0.0 1023.3 jit_solution(5435945143011410280)
XLA Ops:
  0.6 0.7 copy.27
  1.3 1.0 reshape.188
  2.3 0.7 maximum_bitcast_fusion.refs_8_
  3.0 4.3 turn.1
  7.3 612.1 %reduce_scatter.1 = (f32[36288,128]{1,0:T(8,128)}, f32[8,128]{1,0:T(8,128)}, bf16[217728,128]{1,0:T(8,128)(2,1)}) custom-call(bf16[122880,128]{1,0:T(8,128)(2,1)} %bitcast.134, bf16[11520,128]{1,0:T(8,128)(2,1)} %bitcast.147, bf16[5760,128]{1,0:T(8,128)(2,1)} %bitcast.151, bf16[5760,128]{1,0:T(8,128)(2,1)} %bitcast.146, bf16[11520,128]{1,0:T(8,128)(2,1)} %bitcast.148, ...), custom_call_target="tpu_custom_call" | custom-call | tf_op jit(solution)/shard_map/reduce_scatter/pallas_call | solution.py:323
  619.4 315.6 %step_and_gather.1 = (f32[35973,128]{1,0:T(8,128)}, f32[35973,128]{1,0:T(8,128)}, f32[35973,128]{1,0:T(8,128)}, bf16[36288,8,128]{2,1,0:T(8,128)(2,1)}) custom-call(f32[5]{0:T(128)} %scal.1, f32[4536,8,128]{2,1,0:T(8,128)} %bitcast.135, f32[8,128]{1,0:T(8,128)} %get-tuple-element.34.sq_ref, f32[35973,128]{1,0:T(8,128)} %bitcast.136, f32[35973,128]{1,0:T(8,128)} %bitcast.137, ...), custom_call_target="tpu_custom_call" | custom-call | tf_op jit(solution)/shard_map/step_and_gather/pallas_call | solution.py:627
  935.0 0.7 slice.13
  935.7 0.6 reshape.218
  936.3 0.9 slice.12
  937.2 48.7 %unpack.1 = (bf16[15360,8,128]{2,1,0:T(8,128)(2,1)}, bf16[1440,8,128]{2,1,0:T(8,128)(2,1)}, bf16[720,8,128]{2,1,0:T(8,128)(2,1)}, bf16[720,8,128]{2,1,0:T(8,128)...) custom-call(bf16[36288,8,128]{2,1,0:T(8,128)(2,1)} %get-tuple-elemen, ...), custom_call_target="tpu_custom_call" | custom-call | tf_op jit(solution)/shard_map/unpack/pallas_call | solution.py:786
  985.9 0.7 reshape.217
  986.6 0.0 copy-start
  986.6 0.0 slice-start
  986.6 0.0 slice-start.2
  986.6 16.2 %copy.31 = f32[4604544]{0:T(1024)} copy(f32[4604544]{0:T(1024)} %bitcast.143) | data formatting | bytes 36836352
  1002.8 2.0 copy-done
  1004.8 0.0 slice-start.3
  1004.8 9.2 copy.32
  1014.1 0.0 slice-done
  1014.1 0.0 slice-done.1
  1014.1 0.0 slice-done.2
  1014.1 2.1 slice-done.3
  1016.2 0.4 slice-done.4
  1016.6 6.7 copy.33
  (4 shorter events, 0.0 us)
Async XLA Ops:
  986.6 18.2 %copy-start = (f32[35973,128]{1,0:T(8,128)S(1)}, f32[35973,128]{1,0:T(8,128)}, u32[]{:S(2)}) copy-start(f32[35973,128]{1,0:T(8,128)} %get-tuple-element.45) | copy-start | bytes 55254532
  986.6 27.4 %slice-start = ((s8[18419712]{0:T(1024)(128)(4,1)}), s8[4194304]{0:T(1024)(128)(4,1)S(1)}, s32[]{:S(2)}) async-start(s8[18419712]{0:T(1024)(128)(4,1)} %bitcast.139), calls=%async_computation | async-start | bytes 8388608
  986.6 27.4 %slice-start.1 = ((s8[18419712]{0:T(1024)(128)(4,1)}), s8[4194304]{0:T(1024)(128)(4,1)S(1)}, s32[]{:S(2)}) async-start(s8[18419712]{0:T(1024)(128)(4,1)} %bitcast.139), calls=%async_computation.1 | async-start | bytes 8388608
  986.6 27.4 %slice-start.2 = ((s8[18419712]{0:T(1024)(128)(4,1)}), s8[4194304]{0:T(1024)(128)(4,1)S(1)}, s32[]{:S(2)}) async-start(s8[18419712]{0:T(1024)(128)(4,1)} %bitcast.139), calls=%async_computation.2 | async-start | bytes 8388608
  1004.8 11.4 %slice-start.3 = ((s8[18419712]{0:T(1024)(128)(4,1)}), s8[4194304]{0:T(1024)(128)(4,1)S(1)}, s32[]{:S(2)}) async-start(s8[18419712]{0:T(1024)(128)(4,1)} %bitcast.139), calls=%async_computation.3 | async-start | bytes 8388608
  1004.8 11.8 %slice-start.4 = ((s8[18419712]{0:T(1024)(128)(4,1)}), s8[1642496]{0:T(1024)(128)(4,1)S(1)}, s32[]{:S(2)}) async-start(s8[18419712]{0:T(1024)(128)(4,1)} %bitcast.139), calls=%async_computation.4 | async-start | bytes 3284992

commit v6 on v5

--- a/solution.py
+++ b/solution.py
@@ -252,6 +252,9 @@
     @pl.loop(0, NCH)
     def _(k):
         for d in range(2):
+            for q in range(2):
+                for slot in range(3):
+                    hop(d, q, slot, k).wait_send()
             ready(d, 1, k)
             pass_on(d, k).wait_recv()
 
@@ -279,14 +282,6 @@
     sq_all[pl.ds(pl.multiple_of(me * SB, SB), SB), :] = accum[...]
     for d in range(2):
         out_copy(d, NCH - 1).wait()
-    for d in range(2):
-        @pl.loop(0, NCH)
-        def _(k):
-            for q in range(2):
-                for slot in range(3):
-                    hop(d, q, slot, k).wait_send()
-            pass_on(d, k).wait_send()
-
     def tell(step):
         return pltpu.make_async_remote_copy(
             src_ref=accum, dst_ref=sq_all.at[pl.ds(pl.multiple_of(me * SB, SB), SB)],
@@ -295,6 +290,8 @@
 
     for step in range(DEV - 1):
         tell(step).start()
+    for d in range(2):
+        pl.loop(0, NCH)(lambda k, d=d: pass_on(d, k).wait_send())
     for step in range(DEV - 1):
         tell(step).wait()
     whole = sq_all[pl.ds(0, SB), :]
@@ -518,12 +515,9 @@
             copy(kind, i % 2, i // 2).start()
         keep(i).start()
 
-    @pl.when(b == 0)
-    def _():
-        barrier_all(me)
-
     for i in range(PIECES_OUT):
         pl.when(b == by_owner(me, np.maximum(NEED[i] - 3, 0)))(lambda i=i: take(i).start())
+    pl.when(b == 0)(lambda: barrier_all(me))
     made = [by_owner(me, MADE[i]) for i in range(PIECES_OUT)]
     for i in range(PIECES_OUT):
         pl.when(b == made[i] + 1)(functools.partial(give, i))
@@ -602,20 +596,26 @@
             copy(1, 0, k).wait_recv()
             copy(5, 0, k).start()
 
+        def finish(k):
+            for d in range(2):
+                copy(6, d, k).wait_recv()
+                copy(3, d, k).wait_send()
+                copy(6, d, k).wait_send()
+
         @pl.loop(0, ACH)
         def _(k):
             for d in range(2):
                 copy(3, d, k).wait_recv()
                 copy(6, d, k).start()
-
-        @pl.loop(0, ACH)
-        def _(k):
             for d in range(2):
-                for kind in (2, 4, 5, 6):
+                for kind in (2, 4, 5):
                     copy(kind, d, k).wait_recv()
-                for kind in range(7):
+                for kind in (0, 1, 2, 4, 5):
                     copy(kind, d, k).wait_send()
                 keep(2 * k + d).wait()
+            pl.when(k > 1)(lambda: finish(jnp.where(k > 1, k - 2, 0)))
+
+        pl.loop(ACH - 2, ACH)(finish)
 
 
 def step_and_gather(scal, g, sq, m, v, p):

time: 1030 us -> 1020 us (level)
  no operation moved by 1% of the time
where the time goes in v6:
time: 1020 us
  Pallas kernels  979 us (96%)
  local copies, waits for them, and re-layouts  41.3 us (4%)
    pallas_call x1, Pallas kernels, reduce_scatter(): pl.pallas_call(rs_kernel, name='reduce_scatter', out_shape=(jax.ShapeDtyp...  612 us
    pallas_call x1, Pallas kernels, step_and_gather(): pl.pallas_call(step_kernel, name='step_and_gather', grid_spec=pltpu.Prefe...  314 us
    pallas_call x1, Pallas kernels, unpack(): pl.pallas_call(unpack_kernel, name='unpack', out_shape=[jax.ShapeDtypeStr...  48.7 us
    unnamed x16, local copies, waits for them, and re-layouts  37.4 us

profile of v6, /device:TPU:0, one launch (start us, length us, event | category | flops | bytes accessed | tf_op | source)
XLA Modules:
  0.0 1021.9 jit_solution(12329079974952719488)
XLA Ops:
  0.6 0.7 copy.27
  1.3 1.0 reshape.188
  2.3 0.7 maximum_bitcast_fusion.refs_8_
  3.0 4.3 turn.1
  7.3 611.9 %reduce_scatter.1 = (f32[36288,128]{1,0:T(8,128)}, f32[8,128]{1,0:T(8,128)}, bf16[217728,128]{1,0:T(8,128)(2,1)}) custom-call(bf16[122880,128]{1,0:T(8,128)(2,1)} %bitcast.134, bf16[11520,128]{1,0:T(8,128)(2,1)} %bitcast.147, bf16[5760,128]{1,0:T(8,128)(2,1)} %bitcast.151, bf16[5760,128]{1,0:T(8,128)(2,1)} %bitcast.146, bf16[11520,128]{1,0:T(8,128)(2,1)} %bitcast.148, ...), custom_call_target="tpu_custom_call" | custom-call | tf_op jit(solution)/shard_map/reduce_scatter/pallas_call | solution.py:320
  619.2 314.4 %step_and_gather.1 = (f32[35973,128]{1,0:T(8,128)}, f32[35973,128]{1,0:T(8,128)}, f32[35973,128]{1,0:T(8,128)}, bf16[36288,8,128]{2,1,0:T(8,128)(2,1)}) custom-call(f32[5]{0:T(128)} %scal.1, f32[4536,8,128]{2,1,0:T(8,128)} %bitcast.135, f32[8,128]{1,0:T(8,128)} %get-tuple-element.34.sq_ref, f32[35973,128]{1,0:T(8,128)} %bitcast.136, f32[35973,128]{1,0:T(8,128)} %bitcast.137, ...), custom_call_target="tpu_custom_call" | custom-call | tf_op jit(solution)/shard_map/step_and_gather/pallas_call | solution.py:627
  933.5 0.7 slice.13
  934.2 0.6 reshape.218
  934.8 0.9 slice.12
  935.8 48.7 %unpack.1 = (bf16[15360,8,128]{2,1,0:T(8,128)(2,1)}, bf16[1440,8,128]{2,1,0:T(8,128)(2,1)}, bf16[720,8,128]{2,1,0:T(8,128)(2,1)}, bf16[720,8,128]{2,1,0:T(8,128)...) custom-call(bf16[36288,8,128]{2,1,0:T(8,128)(2,1)} %get-tuple-elemen, ...), custom_call_target="tpu_custom_call" | custom-call | tf_op jit(solution)/shard_map/unpack/pallas_call | solution.py:786
  984.5 0.7 reshape.217
  985.2 0.0 copy-start
  985.2 0.0 slice-start
  985.2 0.0 slice-start.1
  985.2 0.0 slice-start.2
  985.2 16.2 %copy.31 = f32[4604544]{0:T(1024)} copy(f32[4604544]{0:T(1024)} %bitcast.143) | data formatting | bytes 36836352
  1001.4 2.0 copy-done
  1003.4 9.2 copy.32
  1012.6 0.0 slice-done
  1012.6 0.0 slice-done.1
  1012.6 0.0 slice-done.2
  1012.6 2.1 slice-done.3
  1014.8 0.4 slice-done.4
  1015.2 6.7 copy.33
  (4 shorter events, 0.0 us)
Async XLA Ops:
  985.2 18.2 %copy-start = (f32[35973,128]{1,0:T(8,128)S(1)}, f32[35973,128]{1,0:T(8,128)}, u32[]{:S(2)}) copy-start(f32[35973,128]{1,0:T(8,128)} %get-tuple-element.45) | copy-start | bytes 55254532
  985.2 27.4 %slice-start = ((s8[18419712]{0:T(1024)(128)(4,1)}), s8[4194304]{0:T(1024)(128)(4,1)S(1)}, s32[]{:S(2)}) async-start(s8[18419712]{0:T(1024)(128)(4,1)} %bitcast.139), calls=%async_computation | async-start | bytes 8388608
  985.2 27.4 %slice-start.1 = ((s8[18419712]{0:T(1024)(128)(4,1)}), s8[4194304]{0:T(1024)(128)(4,1)S(1)}, s32[]{:S(2)}) async-start(s8[18419712]{0:T(1024)(128)(4,1)} %bitcast.139), calls=%async_computation.1 | async-start | bytes 8388608
  985.2 27.4 %slice-start.2 = ((s8[18419712]{0:T(1024)(128)(4,1)}), s8[4194304]{0:T(1024)(128)(4,1)S(1)}, s32[]{:S(2)}) async-start(s8[18419712]{0:T(1024)(128)(4,1)} %bitcast.139), calls=%async_computation.2 | async-start | bytes 8388608
  1003.4 11.4 %slice-start.3 = ((s8[18419712]{0:T(1024)(128)(4,1)}), s8[4194304]{0:T(1024)(128)(4,1)S(1)}, s32[]{:S(2)}) async-start(s8[18419712]{0:T(1024)(128)(4,1)} %bitcast.139), calls=%async_computation.3 | async-start | bytes 8388608
  1003.4 11.8 %slice-start.4 = ((s8[18419712]{0:T(1024)(128)(4,1)}), s8[1642496]{0:T(1024)(128)(4,1)S(1)}, s32[]{:S(2)}) async-start(s8[18419712]{0:T(1024)(128)(4,1)} %bitcast.139), calls=%async_computation.4 | async-start | bytes 3284992
